TPU v7x, 32 devices: a whole 2x2x4 slice. The times are simulated.
32 devices in a mesh: facet: 16 (over z, x, core), col: 2 (over y).
Axes of the slice: x: 2, y: 2, z: 4, core: 2. Of those that a mesh axis runs over, the one named last changes fastest.
Arguments:
- facet_strips: bfloat16 [16, 2, 8192, 128], P('facet', None, 'col'), may hold values from -6 to 6
- facet_offsets: int32 [16, 2], P('facet'), may hold values from 0 to 65535
- column_offsets: int32 [2], P('col'), may hold values from 0 to 65535
- row_offsets: int32 [1], replicated, may hold values from 0 to 65535
- tile_lists: int32 [2, 16, 8], P('col', 'facet'), may hold values from 0 to 63
- tile_counts: int32 [2, 16], P('col', 'facet'), may hold values from 1 to 8, 64 in all within a row
- uv_index: int32 [2, 16, 8, 2, 1024], P('col', 'facet'), may hold values from 0 to 4095
Outputs:
- visibilities: float32 [2, 16, 8, 2, 1024], P('col', 'facet')
Inputs may be any that keep to these rules, and one draw needn't show every extreme that they name: `tile_counts`: each column has an owner whose count is exactly 8.
All inputs are finite; a program needn't handle non-finite values. No bound on the sum of `tile_counts` on one device may be relied on, other than what follows from the above.
Results may differ from a plain program's by a relative error of at most 0.0058.
Values may be sent and summed in bfloat16 or wider, within the bound.
No kernel may reach another device: no remote copies, remote signals or barrier semaphores. Data moves between devices by JAX's collectives and lax.ppermute only.
A program may use at most 64 MiB of HBM per device.

v0:
```python
import math

import jax
import jax.numpy as jnp
from jax import lax
from jax.sharding import PartitionSpec as P

L = 8192
W = 128
S = 256
TILE = 32
NTOT = 65536
UV_STEPS = 4096


def mod_product(first, second):
    high = first // 256
    low = first % 256
    return (high * (second * 256 % NTOT) + low * second) % NTOT


def phase_parts(row_start, row_count, row_step, col_start, col_count, col_step):
    left_side = ((row_start + row_step * jnp.arange(row_count, dtype=jnp.int32)) % NTOT)[:, None]
    right_side = ((col_start + col_step * jnp.arange(col_count, dtype=jnp.int32)) % NTOT)[None, :]
    index = mod_product(left_side, right_side)
    angle = index.astype(jnp.float32) * (2.0 * math.pi / NTOT)
    return (jnp.cos(angle), jnp.sin(angle))


def left_operator(row_start, col_start, count):
    cosine, sine = phase_parts(row_start, S, NTOT // L, col_start, count, 1)
    upper = jnp.concatenate([cosine, sine], axis=1)
    lower = jnp.concatenate([-sine, cosine], axis=1)
    return (jnp.concatenate([upper, lower], axis=0) * (1.0 / math.sqrt(L))).astype(jnp.bfloat16)


def right_operator(column_start, strip_start):
    cosine, sine = phase_parts(strip_start, W, 1, column_start, S, NTOT // S)
    table = jnp.stack([jnp.stack([cosine, -sine], axis=1), jnp.stack([sine, cosine], axis=1)])
    table = table * (1.0 / math.sqrt(W))
    return table.reshape(2, W, 2, S // TILE, TILE).astype(jnp.bfloat16)


def tile_terms(strip_rows, table):
    count = strip_rows.shape[0]
    shaped = strip_rows.reshape(count, 2, S // TILE, TILE, W)
    terms = jnp.einsum("rkapw,kwjbq->abrjpq", shaped, table, preferred_element_type=jnp.float32)
    return terms.reshape((S // TILE) ** 2, count, 2, TILE * TILE)


def visibilities_of(chosen, uv_slots):
    slots = chosen.shape[0]
    tiles = chosen.astype(jnp.float32).reshape(slots, 2, TILE, TILE)
    pixels = jnp.arange(TILE, dtype=jnp.int32)
    factor = 2.0 * math.pi / UV_STEPS
    u_angle = (uv_slots[:, 0, None, :] * pixels[None, :, None] % UV_STEPS).astype(
        jnp.float32
    ) * factor
    v_angle = (uv_slots[:, 1, None, :] * pixels[None, :, None] % UV_STEPS).astype(
        jnp.float32
    ) * factor
    u_cos, u_sin = (jnp.cos(u_angle), jnp.sin(u_angle))
    v_cos, v_sin = (jnp.cos(v_angle), jnp.sin(v_angle))
    high = lax.Precision.HIGHEST
    real_mid = jnp.einsum("cpq,cqk->cpk", tiles[:, 0], v_cos, precision=high) - jnp.einsum(
        "cpq,cqk->cpk", tiles[:, 1], v_sin, precision=high
    )
    imag_mid = jnp.einsum("cpq,cqk->cpk", tiles[:, 0], v_sin, precision=high) + jnp.einsum(
        "cpq,cqk->cpk", tiles[:, 1], v_cos, precision=high
    )
    real_vis = jnp.sum(u_cos * real_mid - u_sin * imag_mid, axis=1) / TILE
    imag_vis = jnp.sum(u_cos * imag_mid + u_sin * real_mid, axis=1) / TILE
    return jnp.stack([real_vis, imag_vis], axis=1)


def shards(
    facet_strips, facet_offsets, column_offsets, row_offsets, tile_lists, tile_counts, uv_index
):
    strip = facet_strips[0]
    strip_along = facet_offsets[0, 0]
    strip_across = facet_offsets[0, 1]
    row_total = row_offsets.shape[0]
    first_cell = lax.axis_index("col") * strip.shape[1]
    count = strip.shape[1]
    flat = strip.reshape(2 * count, strip.shape[2])
    parts = [
        jnp.dot(
            left_operator(row_offsets[0], strip_along + first_cell, count),
            flat,
            preferred_element_type=jnp.float32,
        )
    ]
    summed_rows = lax.psum(jnp.stack(parts), "col")
    strip_rows = summed_rows.astype(jnp.bfloat16)
    table = right_operator(column_offsets[0], strip_across)
    terms = tile_terms(strip_rows, table) * (1.0 / math.sqrt(lax.axis_size("facet")))
    identity = tile_lists[0, 0]
    live = tile_counts[0, 0]
    slot_index = jnp.arange(identity.shape[0], dtype=jnp.int32)
    id_count = terms.shape[0] * row_total
    onehot = (
        (identity[:, None] == jnp.arange(id_count, dtype=jnp.int32)[None, :])
        & (slot_index[:, None] < live)
    ).astype(jnp.bfloat16)
    width = 2 * TILE * TILE
    owned = lax.psum_scatter(terms, "facet", scatter_dimension=0, tiled=True).astype(jnp.bfloat16)
    piece = lax.all_gather(owned, "facet", axis=0, tiled=True)
    count = piece.shape[0]
    flat = piece.reshape(count * row_total, width)
    chosen = jnp.dot(onehot, flat, preferred_element_type=jnp.float32)
    chosen = chosen.astype(jnp.bfloat16).reshape(identity.shape[0], 2, TILE * TILE)
    result = visibilities_of(chosen, uv_index[0, 0])
    return result[None, None]


def solution(mesh):
    in_specs = (
        P("facet", None, "col", None),
        P("facet", None),
        P("col"),
        P(),
        P("col", "facet", None),
        P("col", "facet"),
        P("col", "facet", None, None, None),
    )
    out_specs = P("col", "facet", None, None, None)
    return jax.shard_map(shards, mesh=mesh, in_specs=in_specs, out_specs=out_specs, check_vma=False)
```

profile of v0, /device:TPU:0, one launch (start us, length us, event | category | flops | bytes accessed | tf_op | source)
XLA Modules:
  0.0 166.0 jit_solution(12459840648595184371)
XLA Ops:
  0.0 0.0 copy-start
  0.0 1.4 fusion.79
  2.7 18.4 %fusion.6 = (f32[256,4096]{1,0:T(8,128)S(1)}, f32[256,4096]{1,0:T(8,128)}, f32[256,4096]{1,0:T(8,128)}) fusion(s32[4096]{0:T(1024)S(1)} %get-tuple-element.20, s32[256]{0:T(256)S(1)} %get-tuple-element.21, s32[4096]{0:T(1024)S(1)} %get-tuple-element.19, s32[256]{0:T(256)S(1)} %get-tuple-element.22), kind=kLoop, calls=%fused_computation.9 | loop fusion | flops 17825792 | bytes 12617728 | tf_op jit(solution)/shard_map/sin | solution.py:27
  21.1 10.0 %fusion.9 = f32[1,512,128]{2,1,0:T(8,128)S(1)} fusion(bf16[8192,128]{1,0:T(8,128)(2,1)S(1)} %bitcast.67, f32[256,4096]{1,0:T(8,128)} %get-tuple-element.10, f32[256,4096]{1,0:T(8,128)} %get-tuple-element.11, f32[256,4096]{1,0:T(8,128)S(1)} %get-tuple-element.9), kind=kOutput, calls=%fused_computation.22 | convolution fusion | flops 1094713344 | bytes 14942208 | tf_op jit(solution)/shard_map/dot_general | solution.py:87
  31.1 13.0 %all-reduce.3 = bf16[1,512,128]{2,1,0:T(8,128)(2,1)S(1)} all-reduce(f32[1,512,128]{2,1,0:T(8,128)S(1)} %fusion.9), channel_id=1, replica_groups=mesh['facet'=16,'col'=2] {'col'}, use_global_device_ids=true, to_apply=%region_0.1 | all-reduce | flops 65536 | bytes 393216 | tf_op jit(solution)/shard_map/psum | solution.py:93
  44.1 0.7 and_select_fusion.3
  45.5 0.6 fusion.44
  46.1 1.8 %fusion.8 = f32[8,8,1,2,32,32]{4,5,0,1,3,2:T(8,128)} fusion(bf16[2,8,32,128,1,1]{3,2,1,0,5,4:T(8,128)(2,1)S(1)} %bitcast.70, f32[1,128,1,8,32]{1,4,0,3,2:T(8,128)S(1)} %get-tuple-element.14, f32[1,128,1,8,32]{1,4,0,3,2:T(8,128)S(1)} %get-tuple-element.13, f32[1,128,1,8,32]{1,4,0,3,2:T(8,128)S(1)} %get-tuple-element.12), kind=kOutput, calls=%fused_computation.13 | convolution fusion | flops 67895296 | bytes 1048576 | tf_op jit(solution)/shard_map/rkapw,kwjbq->abrjpq/dot_general | solution.py:47
  47.9 2.9 %copy.24 = f32[8,8,1,2,32,32]{5,4,1,0,3,2:T(8,128)} copy(f32[8,8,1,2,32,32]{4,5,0,1,3,2:T(8,128)} %fusion.8) | data formatting | bytes 1048576 | tf_op jit(solution)/shard_map/mul | solution.py:96
  50.8 2.4 %mul.297 = f32[64,1,2,1024]{3,0,2,1:T(8,128)S(1)} reshape(f32[8,8,1,2,32,32]{5,4,1,0,3,2:T(8,128)} %copy.24) | data formatting | bytes 1048576 | tf_op jit(solution)/shard_map/mul | solution.py:96
  53.3 65.1 %all-reduce.4 = bf16[64,1,2,1024]{3,0,2,1:T(8,128)(2,1)S(1)} all-reduce(f32[64,1,2,1024]{3,0,2,1:T(8,128)S(1)} %mul.297), channel_id=2, replica_groups=mesh['facet'=16,'col'=2] {'facet'}, use_global_device_ids=true, to_apply=%region_1.2.clone | all-reduce | flops 131072 | bytes 786432
  118.4 0.0 copy-done.3
  118.4 0.6 dynamic-slice
  119.7 18.0 %all_gather.3 = bf16[64,1,2,1024]{3,2,1,0:T(2,128)(2,1)S(1)} all-gather(bf16[4,1,2,1024]{3,2,1,0:T(2,128)(2,1)S(1)} %copy.25), channel_id=1, replica_groups=mesh['facet'=16,'col'=2] {'facet'}, dimensions={0}, use_global_device_ids=true | all-gather | bytes 278528 | tf_op jit(solution)/shard_map/all_gather | solution.py:107
  137.7 0.1 copy.40
  138.4 0.0 copy-done.2
  138.4 0.2 convolution_convert_fusion
  138.6 0.2 reshape.493
  138.8 0.1 fusion.78
  138.9 5.6 %fusion.29 = f32[8,32,1024]{2,1,0:T(8,128)S(1)} fusion(s32[8,1024]{1,0:T(8,128)S(1)} %get-tuple-element.17, bf16[8,2,32,32]{3,2,1,0:T(8,128)(2,1)S(1)} %reshape.493), kind=kOutput, calls=%fused_computation.42 | convolution fusion | flops 104333312 | bytes 1146880 | tf_op jit(solution)/shard_map/cpq,cqk->cpk/dot_general | solution.py:65
  144.5 5.7 %convolution_subtract_fusion = f32[8,32,1024]{2,1,0:T(8,128)S(1)} fusion(f32[8,32,1024]{2,1,0:T(8,128)S(1)} %fusion.29, s32[8,1024]{1,0:T(8,128)S(1)} %get-tuple-element.17, bf16[8,2,32,32]{3,2,1,0:T(8,128)(2,1)S(1)} %reshape.493), kind=kOutput, calls=%fused_computation.21 | convolution fusion | flops 104595456 | bytes 2195456 | tf_op jit(solution)/shard_map/cpq,cqk->cpk/dot_general | solution.py:65
  150.2 5.6 %fusion.31 = f32[8,32,1024]{2,1,0:T(8,128)S(1)} fusion(s32[8,1024]{1,0:T(8,128)S(1)} %get-tuple-element.17, bf16[8,2,32,32]{3,2,1,0:T(8,128)(2,1)S(1)} %reshape.493), kind=kOutput, calls=%fused_computation.43 | convolution fusion | flops 104333312 | bytes 1146880 | tf_op jit(solution)/shard_map/cpq,cqk->cpk/dot_general | solution.py:68
  155.8 9.4 %subtract_reduce_fusion = (f32[8,1024]{1,0:T(8,128)S(1)}, f32[8,1024]{1,0:T(8,128)S(1)}) fusion(f32[8,32,1024]{2,1,0:T(8,128)S(1)} %convolution_subtract_fusion, s32[8,1024]{1,0:T(8,128)S(1)} %get-tuple-element.18, f32[8,32,1024]{2,1,0:T(8,128)S(1)} %fusion.31, s32[8,1024]{1,0:T(8,128)S(1)} %get-tuple-element.17, bf16[8,2,32,32]{3,2,1,0:T(8,128)(2,1)S(1)} %reshape.493), kind=kOutput, calls=%fused_computation.30 | convolution fusion | flops 110346240 | bytes 2293760 | tf_op jit(solution)/shard_map/cpq,cqk->cpk/dot_general | solution.py:68
  165.3 0.7 maximum_bitcast_fusion
  (16 shorter events, 0.2 us)
Async XLA Ops:
  0.0 21.1 %copy-start = (bf16[1,2,4096,128]{3,2,1,0:T(8,128)(2,1)S(1)}, bf16[1,2,4096,128]{3,2,1,0:T(8,128)(2,1)}, u32[]{:S(2)}) copy-start(bf16[1,2,4096,128]{3,2,1,0:T(8,128)(2,1)} %param.7) | copy-start | bytes 6291460
  47.9 70.5 %copy-start.3 = (u32[32]{0:T(128)S(1)}, u32[32]{0:T(128)}, u32[]{:S(2)}) copy-start(u32[32]{0:T(128)} %constant.167) | copy-start | bytes 388
  47.9 90.5 %copy-start.2 = (s32[1,1,8]{2,1,0:T(1,128)S(1)}, s32[1,1,8]{2,1,0:T(1,128)}, u32[]{:S(2)}) copy-start(s32[1,1,8]{2,1,0:T(1,128)} %param.11) | copy-start | bytes 100
  47.9 90.9 %copy-start.1 = (s32[1,1,8,2,1024]{4,3,2,1,0:T(2,128)S(1)}, s32[1,1,8,2,1024]{4,3,2,1,0:T(2,128)}, u32[]{:S(2)}) copy-start(s32[1,1,8,2,1024]{4,3,2,1,0:T(2,128)} %param.13) | copy-start | bytes 196612
where the time goes:
time: 166 us
  blocking collectives  96.1 us (58%)
  matrix products  38.2 us (23%)
  other arithmetic  20.5 us (12%)
  local copies, waits for them, and re-layouts  7.72 us (5%)
  between operations  3.44 us (2%)
    unnamed x1, blocking collectives  65.1 us
    sin x1, other arithmetic, phase_parts(): return (jnp.cos(angle), jnp.sin(angle))  18.4 us
    all_gather x1, blocking collectives, shards(): piece = lax.all_gather(owned, 'facet', axis=0, tiled=True)  18 us
    psum x1, blocking collectives, shards(): summed_rows = lax.psum(jnp.stack(parts), 'col')  13 us
    dot_general x1, matrix products, shards(): jnp.dot(left_operator(row_offsets[0], strip_along + first_cell, count), f...  9.98 us
    dot_general x1, matrix products, visibilities_of(): jnp.einsum('cpq,cqk->cpk', tiles[:, 1], v_cos, precision=high)  9.35 us
    dot_general x1, matrix products, visibilities_of(): jnp.einsum('cpq,cqk->cpk', tiles[:, 1], v_sin, precision=high)  5.66 us
    dot_general x1, matrix products, visibilities_of(): jnp.einsum('cpq,cqk->cpk', tiles[:, 0], v_sin, precision=high)  5.63 us

commit v1 on v0

v1 whole, which is shorter than its diff:
```python
import functools
import math

import jax
import jax.numpy as jnp
from jax import lax
from jax.experimental import pallas as pl
from jax.experimental.pallas import tpu as pltpu
from jax.sharding import PartitionSpec as P

L = 8192
W = 128
S = 256
TILE = 32
NTOT = 65536
UV_STEPS = 4096
BF16 = jnp.bfloat16
F32 = jnp.float32
I32 = jnp.int32


def cos_sin(index):
    shifted = index + NTOT // 8
    quadrant = shifted >> 14
    rest = (shifted & (NTOT // 4 - 1)) - NTOT // 8
    x = rest.astype(F32) * (2.0 * math.pi / NTOT)
    y = x * x
    sine = x + x * (y * (-1.0 / 6 + y * (1.0 / 120 + y * (-1.0 / 5040 + y * (1.0 / 362880)))))
    cosine = 1.0 + y * (-0.5 + y * (1.0 / 24 + y * (-1.0 / 720 + y * (1.0 / 40320))))
    odd = (quadrant & 1) != 0
    first = jnp.where(odd, sine, cosine)
    second = jnp.where(odd, cosine, sine)
    return (
        jnp.where(((quadrant + 1) & 2) != 0, -first, first),
        jnp.where((quadrant & 2) != 0, -second, second),
    )


def mod_phase(first, second):
    return (first * second) & (NTOT - 1)


def along_kernel(facets, cols, chunk, scal, strip, out, held, table, total, sems):
    count = held.shape[1]
    blocks = count // W
    steps = count // chunk
    copies = []
    for n in range(steps):
        part = pl.ds(n * chunk, chunk)
        copies.append(pltpu.make_async_copy(strip.at[:, part], held.at[:, part], sems.at[n]))
        copies[n].start()
    row_start, col_start, across = scal[0], scal[1], scal[2]
    row = row_start + (NTOT // L) * lax.broadcasted_iota(I32, (S, W), 0)
    lane = lax.broadcasted_iota(I32, (S, W), 1)
    cos_in, sin_in = cos_sin(mod_phase(row, lane))
    cos_out, sin_out = cos_sin(mod_phase(row, col_start + W * lane))
    scale = 1.0 / math.sqrt(L)
    cos_out = cos_out * scale
    sin_out = sin_out * scale
    for n in range(steps):
        for local in range(chunk // W):
            a = n * (chunk // W) + local
            c = cos_out[:, a : a + 1]
            s = sin_out[:, a : a + 1]
            place = slice(local * W, (local + 1) * W)
            table[n % 2, 0:S, place] = (c * cos_in - s * sin_in).astype(BF16)
            table[n % 2, S : 2 * S, place] = (s * cos_in + c * sin_in).astype(BF16)
        copies[n].wait()
        part = slice(n * chunk, (n + 1) * chunk)
        cells = jnp.concatenate([held[0, part, :], held[1, part, :]], axis=1)
        term = jnp.dot(table[n % 2], cells, preferred_element_type=F32)
        if n == 0:
            total[...] = term
        else:
            total[...] += term
    rows = S // facets
    real = total[0:S, 0:W] + total[S : 2 * S, W : 2 * W]
    imag = total[0:S, W : 2 * W] - total[S : 2 * S, 0:W]
    total[0:S, 0:W] = real
    total[0:S, W : 2 * W] = imag
    extra = out.shape[2] - 2 * rows
    high = across >> 8
    low = across & 255
    note = jnp.where(
        lax.broadcasted_iota(I32, (extra, W), 0) == 0, high, low
    ).astype(F32).astype(BF16)
    for o in range(facets):
        re = total[o * rows : (o + 1) * rows, 0:W].astype(BF16)
        im = total[o * rows : (o + 1) * rows, W : 2 * W].astype(BF16)
        for c in range(cols):
            out[o, c, 0:rows, :] = re
            out[o, c, rows : 2 * rows, :] = im
            out[o, c, 2 * rows :, :] = note


def along(strip, scalars, facets, cols):
    count = strip.shape[1]
    chunk = min(1024, count)
    rows = S // facets
    return pl.pallas_call(
        functools.partial(along_kernel, facets, cols, chunk),
        out_shape=jax.ShapeDtypeStruct((facets, cols, 2 * rows + 8, W), BF16),
        in_specs=[
            pl.BlockSpec(memory_space=pltpu.SMEM),
            pl.BlockSpec(memory_space=pl.ANY),
        ],
        out_specs=pl.BlockSpec(memory_space=pltpu.VMEM),
        scratch_shapes=[
            pltpu.VMEM((2, count, W), BF16),
            pltpu.VMEM((2, 2 * S, chunk), BF16),
            pltpu.VMEM((2 * S, 2 * W), F32),
            pltpu.SemaphoreType.DMA((count // chunk,)),
        ],
        cost_estimate=pl.CostEstimate(
            flops=8 * S * W * count, bytes_accessed=4 * count * W, transcendentals=0
        ),
        name="along",
    )(scalars, strip)


def across_kernel(facets, cols, scal, got, out, left, summed):
    rows = S // facets
    column = scal[0]
    wide = 2 * S
    cell = lax.broadcasted_iota(I32, (W, wide), 0)
    lane = lax.broadcasted_iota(I32, (W, wide), 1)
    sample = (lane >> 6) * TILE + (lane & (TILE - 1))
    turn = ((lane >> 5) & 1) * (NTOT // 4)
    position = column + (NTOT // S) * sample
    top, bottom = cos_sin((cell * position + turn) & (NTOT - 1))
    scale = 1.0 / math.sqrt(W)
    right = jnp.concatenate([(top * scale).astype(BF16), (bottom * scale).astype(BF16)], axis=0)
    height = facets * rows
    for f in range(facets):
        re = got[f, 0, 0:rows, :].astype(F32)
        im = got[f, 0, rows : 2 * rows, :].astype(F32)
        for h in range(1, cols):
            re = re + got[f, h, 0:rows, :].astype(F32)
            im = im + got[f, h, rows : 2 * rows, :].astype(F32)
        left[f * rows : (f + 1) * rows, 0:W] = re
        left[f * rows : (f + 1) * rows, W : 2 * W] = im
        left[height + f * rows : height + (f + 1) * rows, 0:W] = im
        left[height + f * rows : height + (f + 1) * rows, W : 2 * W] = -re
    summed[...] = jnp.dot(left[...].astype(BF16), right, preferred_element_type=F32)
    acc = jnp.zeros((rows, wide), F32)
    for f in range(facets):
        note = got[f, 0, 2 * rows : 2 * rows + 8, :].astype(F32)
        offset = (note[0:1, 0:1] * 256.0 + note[1:2, 0:1]).astype(I32)
        cosine, sine = cos_sin(mod_phase(offset, position[0:1, :]))
        acc = acc + summed[f * rows : (f + 1) * rows, :] * cosine
        acc = acc + summed[height + f * rows : height + (f + 1) * rows, :] * sine
    acc = (acc * (1.0 / math.sqrt(facets))).astype(BF16)
    for o in range(facets):
        for m in range(wide // W):
            out[o, m] = acc[:, m * W : (m + 1) * W]


def across(got, scalars, facets, cols):
    rows = S // facets
    return pl.pallas_call(
        functools.partial(across_kernel, facets, cols),
        out_shape=jax.ShapeDtypeStruct((facets, 2 * S // W, rows, W), BF16),
        in_specs=[
            pl.BlockSpec(memory_space=pltpu.SMEM),
            pl.BlockSpec(memory_space=pltpu.VMEM),
        ],
        out_specs=pl.BlockSpec(memory_space=pltpu.VMEM),
        scratch_shapes=[
            pltpu.VMEM((2 * S, 2 * W), F32),
            pltpu.VMEM((2 * S, 2 * S), F32),
        ],
        cost_estimate=pl.CostEstimate(
            flops=2 * 2 * S * 2 * W * 2 * S, bytes_accessed=1 << 20, transcendentals=0
        ),
        name="across",
    )(scalars, got)


def visibility_kernel(facets, names, live, grid, uv, out, tile, right):
    rows = S // facets
    pieces = TILE // rows
    vis = uv.shape[2]
    step = NTOT // UV_STEPS
    sublane = lax.broadcasted_iota(I32, (TILE, vis), 0) * step
    lane = lax.broadcasted_iota(I32, (TILE, W), 1)
    sign = jnp.where((lane & TILE) == 0, 1.0, -1.0).astype(F32)

    def slot(j, carry):
        @pl.when(j < live[0])
        def _():
            name = names[j]
            a, b = name >> 3, name & 7
            for t in range(pieces):
                tile[t * rows : (t + 1) * rows, :] = grid[a * pieces + t, b >> 1].astype(F32)
            x = tile[...]
            y = pltpu.roll(x, 2 * TILE, 1)
            both = jnp.where((lane >= 2 * TILE) == ((b & 1) == 1), x, y)
            turned = pltpu.roll(both, TILE, 1)
            lhs = jnp.concatenate([both * sign, turned], axis=0).astype(BF16)
            cosine, sine = cos_sin((uv[j, 1:2, :] * sublane) & (NTOT - 1))
            cos_high, sin_high = cosine.astype(BF16), sine.astype(BF16)
            right[0:TILE, :] = cos_high
            right[TILE : 2 * TILE, :] = sin_high
            right[2 * TILE : 3 * TILE, :] = (cosine - cos_high.astype(F32)).astype(BF16)
            right[3 * TILE : 4 * TILE, :] = (sine - sin_high.astype(F32)).astype(BF16)
            middle = jnp.dot(lhs, right[...], preferred_element_type=F32)
            real, imag = middle[0:TILE], middle[TILE : 2 * TILE]
            cosine, sine = cos_sin((uv[j, 0:1, :] * sublane) & (NTOT - 1))
            scale = 1.0 / TILE
            out[j, 0:1, :] = jnp.sum(cosine * real - sine * imag, axis=0, keepdims=True) * scale
            out[j, 1:2, :] = jnp.sum(cosine * imag + sine * real, axis=0, keepdims=True) * scale

        @pl.when(j >= live[0])
        def _():
            out[j] = jnp.zeros((2, vis), F32)

        return carry

    lax.fori_loop(0, uv.shape[0], slot, 0)


def visibilities_of(grid, names, live, uv, facets):
    slots, _, vis = uv.shape
    return pl.pallas_call(
        functools.partial(visibility_kernel, facets),
        out_shape=jax.ShapeDtypeStruct((slots, 2, vis), F32),
        in_specs=[
            pl.BlockSpec(memory_space=pltpu.SMEM),
            pl.BlockSpec(memory_space=pltpu.SMEM),
            pl.BlockSpec(memory_space=pltpu.VMEM),
            pl.BlockSpec(memory_space=pltpu.VMEM),
        ],
        out_specs=pl.BlockSpec(memory_space=pltpu.VMEM),
        scratch_shapes=[
            pltpu.VMEM((TILE, W), F32),
            pltpu.VMEM((4 * TILE, vis), BF16),
        ],
        cost_estimate=pl.CostEstimate(
            flops=slots * 2 * 64 * 128 * vis, bytes_accessed=1 << 20, transcendentals=0
        ),
        name="visibility",
    )(names, live, grid, uv)


def shards(
    facet_strips, facet_offsets, column_offsets, row_offsets, tile_lists, tile_counts, uv_index
):
    facets, cols = lax.axis_size("facet"), lax.axis_size("col")
    strip = facet_strips[0]
    first_cell = lax.axis_index("col") * strip.shape[1]
    scalars = jnp.stack(
        [row_offsets[0], facet_offsets[0, 0] + first_cell, facet_offsets[0, 1]]
    ).astype(I32)
    sent = along(strip, scalars, facets, cols)
    flat = sent.reshape((facets * cols,) + sent.shape[2:])
    got = lax.all_to_all(flat, ("facet", "col"), 0, 0)
    owned = across(got.reshape(sent.shape), column_offsets, facets, cols)
    grid = lax.all_to_all(owned, "facet", 0, 0)
    result = visibilities_of(grid, tile_lists[0, 0], tile_counts[0], uv_index[0, 0], facets)
    return result[None, None]


def solution(mesh):
    in_specs = (
        P("facet", None, "col", None),
        P("facet", None),
        P("col"),
        P(),
        P("col", "facet", None),
        P("col", "facet"),
        P("col", "facet", None, None, None),
    )
    out_specs = P("col", "facet", None, None, None)
    return jax.shard_map(shards, mesh=mesh, in_specs=in_specs, out_specs=out_specs, check_vma=False)
```

time: 166 us -> 50.8 us (0.31)
  blocking collectives: 96.1 us -> 0 us
  matrix products: 38.2 us -> 0 us
  waiting for transfers between devices: 0 us -> 20.4 us
  other arithmetic: 20.5 us -> 1.28 us
  Pallas kernels: 0 us -> 13.4 us
  starting transfers between devices: 0 us -> 10.9 us
  local copies, waits for them, and re-layouts: 7.72 us -> 2.83 us
    unnamed x1 -> x0, blocking collectives: 65.1 us -> none
    dot_general x7 -> x0, matrix products: 38.2 us -> none  [the longest x1 9.98 us: shards(): jnp.dot(left_operator(row_offsets[0], strip_along + first_cell, count), f...]
    all_to_all x0 -> x2, waiting for transfers between devices: none -> 20.4 us  [the longest x1 11.1 us: shards(): got = lax.all_to_all(flat, ('facet', 'col'), 0, 0)]
    sin x1 -> x0, other arithmetic: 18.4 us -> none  [phase_parts(): return (jnp.cos(angle), jnp.sin(angle))]
    all_gather x1 -> x0, blocking collectives: 18 us -> none  [shards(): piece = lax.all_gather(owned, 'facet', axis=0, tiled=True)]
    pallas_call x0 -> x3, Pallas kernels: none -> 13.4 us  [the longest x1 5.45 us: visibilities_of(): pl.pallas_call(functools.partial(visibility_kernel, facets), out_shape=ja...]
    psum x1 -> x0, blocking collectives: 13 us -> none  [shards(): summed_rows = lax.psum(jnp.stack(parts), 'col')]
    all_to_all x0 -> x2, starting transfers between devices: none -> 10.9 us  [the longest x1 7.33 us: shards(): got = lax.all_to_all(flat, ('facet', 'col'), 0, 0)]
  transfers between devices with their start and end apart: 0 -> 2, of which waited for: 0 -> 2; matrix products, arithmetic and copies ran while one was open for 0% -> 0% of each run, Pallas kernels for 0% -> 0%
where the time goes in v1:
time: 50.8 us; the launch traced here: 51.4 us
  waiting for transfers between devices  20.4 us (40%)
  Pallas kernels  13.4 us (26%)
  starting transfers between devices  10.9 us (21%)
  local copies, waits for them, and re-layouts  2.83 us (6%)
  between operations  2.62 us (5%)
  other arithmetic  1.28 us (3%)
    all_to_all x1, waiting for transfers between devices, shards(): got = lax.all_to_all(flat, ('facet', 'col'), 0, 0)  11.1 us
    all_to_all x1, waiting for transfers between devices, shards(): grid = lax.all_to_all(owned, 'facet', 0, 0)  9.33 us
    all_to_all x1, starting transfers between devices, shards(): got = lax.all_to_all(flat, ('facet', 'col'), 0, 0)  7.33 us
    pallas_call x1, Pallas kernels, visibilities_of(): pl.pallas_call(functools.partial(visibility_kernel, facets), out_shape=ja...  5.45 us
    pallas_call x1, Pallas kernels, along(): pl.pallas_call(functools.partial(along_kernel, facets, cols, chunk), out_...  5.32 us
    all_to_all x1, starting transfers between devices, shards(): grid = lax.all_to_all(owned, 'facet', 0, 0)  3.53 us
    pallas_call x1, Pallas kernels, across(): pl.pallas_call(functools.partial(across_kernel, facets, cols), out_shape=...  2.66 us
    unnamed x4, local copies, waits for them, and re-layouts  1.44 us
  transfers between devices with their start and end apart: 2, of which 2 were waited for; matrix products, arithmetic and copies ran while one was open for 0% of the time, Pallas kernels for 0%

profile of v1, /device:TPU:0, one launch (start us, length us, event | category | flops | bytes accessed | tf_op | source)
XLA Modules:
  0.0 51.4 jit_solution(10854498866343895868)
XLA Ops:
  0.0 1.4 %fusion = (s32[1,1]{1,0:T(1,128)}, s32[1,1]{1,0:T(1,128)}) fusion(s32[1,2]{1,0:T(1,128)} %param.8), kind=kLoop, calls=%fused_computation.1 | loop fusion | bytes 16 | tf_op jit(solution)/shard_map/slice | solution.py:252
  2.7 1.3 %pad_add_fusion.scal = s32[3]{0:T(128)} fusion(s32[1]{0:T(128)} %bitcast.4, s32[1]{0:T(128)} %bitcast.3, s32[1]{0:T(128)S(6)} %copy.9), kind=kLoop, calls=%fused_computation | loop fusion | flops 6 | bytes 24 | tf_op jit(solution)/shard_map/stack | solution.py:251
  4.0 5.3 %along.1 = bf16[16,2,40,128]{3,2,1,0:T(8,128)(2,1)} custom-call(s32[3]{0:T(128)} %pad_add_fusion.scal, bf16[2,4096,128]{2,1,0:T(8,128)(2,1)} %bitcast.13), custom_call_target="tpu_custom_call" | custom-call | flops 1073741824 | bytes 2097152 | tf_op jit(solution)/shard_map/along/pallas_call | solution.py:100
  9.3 7.3 %all-to-all-start = ((bf16[32,40,128]{2,1,0:T(8,128)(2,1)}), bf16[32,40,128]{2,1,0:T(8,128)(2,1)S(1)}, u32[]{:S(2)}, u32[]{:S(2)}) async-start(bf16[32,40,128]{2,1,0:T(8,128)(2,1)} %bitcast.12), calls=%async_computation | async-start | bytes 655360 | tf_op jit(solution)/shard_map/all_to_all | solution.py:256
  17.3 11.1 %all-to-all-done = bf16[32,40,128]{2,1,0:T(8,128)(2,1)S(1)} async-done(((bf16[32,40,128]{2,1,0:T(8,128)(2,1)}), bf16[32,40,128]{2,1,0:T(8,128)(2,1)S(1)}, u32[]{:S(2)}, u32[]{:S(2)}) %all-to-all-start) | async-done | bytes 327712 | tf_op jit(solution)/shard_map/all_to_all | solution.py:256
  28.3 0.0 copy-start
  28.3 0.7 %copy-done = bf16[32,40,128]{2,1,0:T(8,128)(2,1)} copy-done((bf16[32,40,128]{2,1,0:T(8,128)(2,1)}, bf16[32,40,128]{2,1,0:T(8,128)(2,1)S(1)}, u32[]{:S(2)}) %copy-start) | copy-done | bytes 327704
  29.1 2.7 %across.1 = bf16[16,4,16,128]{3,2,1,0:T(8,128)(2,1)} custom-call(s32[1]{0:T(128)S(6)} %copy.8.scal, bf16[16,2,40,128]{3,2,1,0:T(8,128)(2,1)} %bitcast.11), custom_call_target="tpu_custom_call" | custom-call | flops 134217728 | bytes 1048576 | tf_op jit(solution)/shard_map/across/pallas_call | solution.py:160
  31.7 3.5 %all-to-all-start.1 = ((bf16[16,4,16,128]{3,2,1,0:T(8,128)(2,1)}), bf16[16,4,16,128]{3,2,1,0:T(8,128)(2,1)S(1)}, u32[]{:S(2)}, u32[]{:S(2)}) async-start(bf16[16,4,16,128]{3,2,1,0:T(8,128)(2,1)} %across.1), calls=%async_computation.1 | async-start | bytes 524288 | tf_op jit(solution)/shard_map/all_to_all | solution.py:258
  35.9 9.3 %all-to-all-done.1.grid = bf16[16,4,16,128]{3,2,1,0:T(8,128)(2,1)S(1)} async-done(((bf16[16,4,16,128]{3,2,1,0:T(8,128)(2,1)}), bf16[16,4,16,128]{3,2,1,0:T(8,128)(2,1)S(1)}, u32[]{:S(2)}, u32[]{:S(2)}) %all-to-all-start.1) | async-done | bytes 262176 | tf_op jit(solution)/shard_map/all_to_all | solution.py:258
  45.3 0.0 copy-start.1
  45.3 0.7 %copy-done.1 = bf16[16,4,16,128]{3,2,1,0:T(8,128)(2,1)} copy-done((bf16[16,4,16,128]{3,2,1,0:T(8,128)(2,1)}, bf16[16,4,16,128]{3,2,1,0:T(8,128)(2,1)S(1)}, u32[]{:S(2)}) %copy-start.1) | copy-done | bytes 262168
  46.0 5.5 %visibility.1 = f32[8,2,1024]{2,1,0:T(2,128)} custom-call(s32[8]{0:T(128)} %bitcast.15, s32[1]{0:T(128)} %bitcast.10.live, bf16[16,4,16,128]{3,2,1,0:T(8,128)(2,1)} %copy-done.1, s32[8,2,1024]{2,1,0:T(2,128)} %bitcast.14), custom_call_target="tpu_custom_call" | custom-call | flops 134217728 | bytes 1048576 | tf_op jit(solution)/shard_map/visibility/pallas_call | solution.py:224
Async XLA Ops:
  9.3 19.0 %all-to-all-start = ((bf16[32,40,128]{2,1,0:T(8,128)(2,1)}), bf16[32,40,128]{2,1,0:T(8,128)(2,1)S(1)}, u32[]{:S(2)}, u32[]{:S(2)}) async-start(bf16[32,40,128]{2,1,0:T(8,128)(2,1)} %bitcast.12), calls=%async_computation | async-start | bytes 655360 | tf_op jit(solution)/shard_map/all_to_all | solution.py:256
  28.3 0.7 %copy-start = (bf16[32,40,128]{2,1,0:T(8,128)(2,1)}, bf16[32,40,128]{2,1,0:T(8,128)(2,1)S(1)}, u32[]{:S(2)}) copy-start(bf16[32,40,128]{2,1,0:T(8,128)(2,1)S(1)} %all-to-all-done) | copy-start | bytes 983044
  31.7 13.5 %all-to-all-start.1 = ((bf16[16,4,16,128]{3,2,1,0:T(8,128)(2,1)}), bf16[16,4,16,128]{3,2,1,0:T(8,128)(2,1)S(1)}, u32[]{:S(2)}, u32[]{:S(2)}) async-start(bf16[16,4,16,128]{3,2,1,0:T(8,128)(2,1)} %across.1), calls=%async_computation.1 | async-start | bytes 524288 | tf_op jit(solution)/shard_map/all_to_all | solution.py:258
  45.3 0.7 %copy-start.1 = (bf16[16,4,16,128]{3,2,1,0:T(8,128)(2,1)}, bf16[16,4,16,128]{3,2,1,0:T(8,128)(2,1)S(1)}, u32[]{:S(2)}) copy-start(bf16[16,4,16,128]{3,2,1,0:T(8,128)(2,1)S(1)} %all-to-all-done.1.grid) | copy-start | bytes 786436

commit v2 on v1

v2 whole, which is shorter than its diff:
```python
import functools
import math

import jax
import jax.numpy as jnp
from jax import lax
from jax.experimental import pallas as pl
from jax.experimental.pallas import tpu as pltpu
from jax.sharding import PartitionSpec as P


L = 8192
W = 128
S = 256
TILE = 32
NTOT = 65536
UV_STEPS = 4096
VMEM_LIMIT = 16 << 20
BF16 = jnp.bfloat16
F32 = jnp.float32
I32 = jnp.int32


def cos_sin(index):
    shifted = index + NTOT // 8
    quadrant = shifted >> 14
    rest = (shifted & (NTOT // 4 - 1)) - NTOT // 8
    x = rest.astype(F32) * (2.0 * math.pi / NTOT)
    y = x * x
    sine = x + x * (y * (-1.0 / 6 + y * (1.0 / 120 + y * (-1.0 / 5040 + y * (1.0 / 362880)))))
    cosine = 1.0 + y * (-0.5 + y * (1.0 / 24 + y * (-1.0 / 720 + y * (1.0 / 40320))))
    odd = (quadrant & 1) != 0
    first = jnp.where(odd, sine, cosine)
    second = jnp.where(odd, cosine, sine)
    return (
        jnp.where(((quadrant + 1) & 2) != 0, -first, first),
        jnp.where((quadrant & 2) != 0, -second, second),
    )


def mod_phase(first, second):
    return (first * second) & (NTOT - 1)


def along_kernel(chunk, rows_at, offsets, strip, rounded, own, held, table, total, sems):
    count = held.shape[1]
    steps = count // chunk
    copies = []
    for n in range(steps):
        part = pl.ds(n * chunk, chunk)
        copies.append(pltpu.make_async_copy(strip.at[:, part], held.at[:, part], sems.at[n]))
        copies[n].start()
    row_start = rows_at[0]
    col_start = offsets[0, 0] + lax.axis_index("col") * count
    row = row_start + (NTOT // L) * lax.broadcasted_iota(I32, (S, W), 0)
    lane = lax.broadcasted_iota(I32, (S, W), 1)
    cos_in, sin_in = cos_sin(mod_phase(row, lane))
    cos_out, sin_out = cos_sin(mod_phase(row, col_start + W * lane))
    scale = 1.0 / math.sqrt(L)
    cos_out = cos_out * scale
    sin_out = sin_out * scale
    for n in range(steps):
        for local in range(chunk // W):
            a = n * (chunk // W) + local
            c = cos_out[:, a : a + 1]
            s = sin_out[:, a : a + 1]
            place = slice(local * W, (local + 1) * W)
            table[n % 2, 0:S, place] = (c * cos_in - s * sin_in).astype(BF16)
            table[n % 2, S : 2 * S, place] = (s * cos_in + c * sin_in).astype(BF16)
        copies[n].wait()
        part = slice(n * chunk, (n + 1) * chunk)
        cells = jnp.concatenate([held[0, part, :], held[1, part, :]], axis=1)
        term = jnp.dot(table[n % 2], cells, preferred_element_type=F32)
        if n == 0:
            total[...] = term
        else:
            total[...] += term
    real = total[0:S, 0:W] + total[S : 2 * S, W : 2 * W]
    imag = total[0:S, W : 2 * W] - total[S : 2 * S, 0:W]
    own[:, 0:W] = real
    own[:, W : 2 * W] = imag
    rounded[:, 0:W] = real.astype(BF16)
    rounded[:, W : 2 * W] = imag.astype(BF16)


def along(strip, row_offsets, facet_offsets):
    count = strip.shape[1]
    chunk = min(1024, count)
    return pl.pallas_call(
        functools.partial(along_kernel, chunk),
        out_shape=(
            jax.ShapeDtypeStruct((S, 2 * W), BF16),
            jax.ShapeDtypeStruct((S, 2 * W), F32),
        ),
        in_specs=[
            pl.BlockSpec(memory_space=pltpu.SMEM),
            pl.BlockSpec(memory_space=pltpu.SMEM),
            pl.BlockSpec(memory_space=pltpu.HBM),
        ],
        out_specs=[pl.BlockSpec(memory_space=pltpu.VMEM)] * 2,
        scratch_shapes=[
            pltpu.VMEM((2, count, W), BF16),
            pltpu.VMEM((2, 2 * S, chunk), BF16),
            pltpu.VMEM((2 * S, 2 * W), F32),
            pltpu.SemaphoreType.DMA((count // chunk,)),
        ],
        compiler_params=pltpu.CompilerParams(vmem_limit_bytes=VMEM_LIMIT),
        cost_estimate=pl.CostEstimate(
            flops=8 * S * W * count, bytes_accessed=4 * count * W, transcendentals=0
        ),
        name="along",
    )(row_offsets, facet_offsets, strip)


def across_kernel(columns, offsets, names, own, other, keep, send, terms):
    facets, slots = names.shape[0], names.shape[2]
    wide = 2 * S
    cell = lax.broadcasted_iota(I32, (W, wide), 0)
    lane = lax.broadcasted_iota(I32, (W, wide), 1)
    sample = (lane >> 6) * TILE + (lane & (TILE - 1))
    turn = ((lane >> 5) & 1) * (NTOT // 4)
    position = columns[0] + (NTOT // S) * sample
    top, bottom = cos_sin(((offsets[0, 1] + cell) * position + turn) & (NTOT - 1))
    scale = 1.0 / math.sqrt(W)
    right = jnp.concatenate([(top * scale).astype(BF16), (bottom * scale).astype(BF16)], axis=0)
    strip_rows = own[...]
    if other is not None:
        strip_rows = strip_rows + other[...].astype(F32)
    product = jnp.dot(strip_rows.astype(BF16), right, preferred_element_type=F32)
    for a in range(S // TILE):
        for m in range(wide // W):
            block = product[a * TILE : (a + 1) * TILE, m * W : (m + 1) * W]
            terms[0, a, m] = block
            terms[1, a, m] = pltpu.roll(block, W // 2, 1)
    core = lax.axis_index("facet") & 1
    first_half = lax.broadcasted_iota(I32, (TILE, W), 1) < W // 2

    def pair(o, slot):
        even, odd = names[o, 0, slot], names[o, 0, slot + 1]
        return jnp.where(
            first_half,
            terms[even & 1, even >> 3, (even & 7) >> 1],
            terms[1 - (odd & 1), odd >> 3, (odd & 7) >> 1],
        )

    def owner(o, carry):
        for n in range(slots // 4):
            keep[o, n] = pair(o, core * (slots // 2) + 2 * n)
            send[o, n] = pair(o, (1 - core) * (slots // 2) + 2 * n).astype(BF16)
        return carry

    lax.fori_loop(0, facets, owner, 0, unroll=4)


def across(own, other, columns, offsets, names):
    facets, _, slots = names.shape
    shape = (facets, slots // 4, TILE, W)
    kernel = across_kernel
    arrays = [own]
    if other is None:
        kernel = lambda c, f, n, own, *rest: across_kernel(c, f, n, own, None, *rest)
    else:
        arrays.append(other)
    return pl.pallas_call(
        kernel,
        out_shape=(jax.ShapeDtypeStruct(shape, F32), jax.ShapeDtypeStruct(shape, BF16)),
        in_specs=[pl.BlockSpec(memory_space=pltpu.SMEM)] * 3
        + [pl.BlockSpec(memory_space=pltpu.VMEM)] * len(arrays),
        out_specs=[pl.BlockSpec(memory_space=pltpu.VMEM)] * 2,
        scratch_shapes=[pltpu.VMEM((2, S // TILE, 2 * S // W, TILE, W), F32)],
        compiler_params=pltpu.CompilerParams(vmem_limit_bytes=VMEM_LIMIT),
        cost_estimate=pl.CostEstimate(
            flops=2 * S * 2 * W * 2 * S, bytes_accessed=1 << 20, transcendentals=0
        ),
        name="across",
    )(columns, offsets, names, *arrays)


def visibility_kernel(live, parts, uv, out, tiles, right):
    facets, pairs = parts.shape[0], parts.shape[1]
    vis = uv.shape[2]
    step = NTOT // UV_STEPS
    sublane = lax.broadcasted_iota(I32, (TILE, vis), 0) * step
    lane = lax.broadcasted_iota(I32, (TILE, W), 1)
    sign = jnp.where((lane & TILE) == 0, 1.0, -1.0).astype(F32)
    scale = 1.0 / math.sqrt(facets)
    for core in range(2):
        for n in range(pairs):
            acc = parts[core, n].astype(F32)
            for f in range(core + 2, facets, 2):
                acc = acc + parts[f, n].astype(F32)
            acc = (acc * scale).astype(BF16).astype(F32)
            turned = pltpu.roll(acc, W // 2, 1)
            tiles[core * 2 * pairs + 2 * n] = jnp.where(lane < W // 2, acc, turned)
            tiles[core * 2 * pairs + 2 * n + 1] = jnp.where(lane < W // 2, turned, acc)

    def slot(j, carry):
        @pl.when(j < live[0, 0])
        def _():
            both = tiles[j]
            turned = pltpu.roll(both, TILE, 1)
            lhs = jnp.concatenate([both * sign, turned], axis=0).astype(BF16)
            cosine, sine = cos_sin((uv[j, 1:2, :] * sublane) & (NTOT - 1))
            cos_high, sin_high = cosine.astype(BF16), sine.astype(BF16)
            right[0:TILE, :] = cos_high
            right[TILE : 2 * TILE, :] = sin_high
            right[2 * TILE : 3 * TILE, :] = (cosine - cos_high.astype(F32)).astype(BF16)
            right[3 * TILE : 4 * TILE, :] = (sine - sin_high.astype(F32)).astype(BF16)
            middle = jnp.dot(lhs, right[...], preferred_element_type=F32)
            real, imag = middle[0:TILE], middle[TILE : 2 * TILE]
            cosine, sine = cos_sin((uv[j, 0:1, :] * sublane) & (NTOT - 1))
            size = 1.0 / TILE
            out[j, 0:1, :] = jnp.sum(cosine * real - sine * imag, axis=0, keepdims=True) * size
            out[j, 1:2, :] = jnp.sum(cosine * imag + sine * real, axis=0, keepdims=True) * size

        @pl.when(j >= live[0, 0])
        def _():
            out[j] = jnp.zeros((2, vis), F32)

        return carry

    lax.fori_loop(0, uv.shape[0], slot, 0)


def visibilities_of(parts, live, uv):
    slots, _, vis = uv.shape
    return pl.pallas_call(
        visibility_kernel,
        out_shape=jax.ShapeDtypeStruct((slots, 2, vis), F32),
        in_specs=[
            pl.BlockSpec(memory_space=pltpu.SMEM),
            pl.BlockSpec(memory_space=pltpu.VMEM),
            pl.BlockSpec(memory_space=pltpu.VMEM),
        ],
        out_specs=pl.BlockSpec(memory_space=pltpu.VMEM),
        scratch_shapes=[
            pltpu.VMEM((slots, TILE, W), F32),
            pltpu.VMEM((4 * TILE, vis), BF16),
        ],
        compiler_params=pltpu.CompilerParams(vmem_limit_bytes=VMEM_LIMIT),
        cost_estimate=pl.CostEstimate(
            flops=slots * 2 * 64 * 128 * vis, bytes_accessed=1 << 20, transcendentals=0
        ),
        name="visibility",
    )(live, parts, uv)


def shards(
    facet_strips, facet_offsets, column_offsets, row_offsets, tile_lists, tile_counts, uv_index
):
    facets, cols = lax.axis_size("facet"), lax.axis_size("col")
    slots = tile_lists.shape[2]
    names = lax.all_to_all(
        jnp.broadcast_to(tile_lists, (facets, 1, slots)), "facet", 0, 0, tiled=True
    )
    rounded, own = along(facet_strips[0], row_offsets, facet_offsets)
    other = None
    if cols == 2:
        other = lax.ppermute(rounded, "col", [(0, 1), (1, 0)])
    else:
        own = lax.psum(own, "col")
    keep, send = across(own, other, column_offsets, facet_offsets, names)
    swapped = lax.ppermute(send, "facet", [(f, f ^ 1) for f in range(facets)])
    both = (keep + swapped.astype(F32)).astype(BF16)
    parts = lax.all_to_all(both, "facet", 0, 0, tiled=True)
    result = visibilities_of(parts, tile_counts, uv_index[0, 0])
    return result[None, None]


def solution(mesh):
    in_specs = (
        P("facet", None, "col", None),
        P("facet", None),
        P("col"),
        P(),
        P("col", "facet", None),
        P("col", "facet"),
        P("col", "facet", None, None, None),
    )
    out_specs = P("col", "facet", None, None, None)
    return jax.shard_map(shards, mesh=mesh, in_specs=in_specs, out_specs=out_specs, check_vma=False)
```

time: 50.8 us -> 43.8 us (0.86); the launches traced: 51.4 us -> 43.2 us
  Pallas kernels: 13.4 us -> 8.36 us
  waiting for transfers between devices: 20.4 us -> 16.6 us
  starting transfers between devices: 10.9 us -> 12.6 us
  between operations: 2.62 us -> 2.03 us
    all_to_all x2, waiting for transfers between devices: 20.4 us -> 15 us  [the longest x1 9.33 us: shards(): parts = lax.all_to_all(both, 'facet', 0, 0, tiled=True)]
    pallas_call x3, Pallas kernels: 13.4 us -> 8.36 us  [the longest x1 4.52 us: along(): pl.pallas_call(functools.partial(along_kernel, chunk), out_shape=(jax.Sha...]
    ppermute x0 -> x2, starting transfers between devices: none -> 3.13 us  [the longest x1 3.06 us: shards(): other = lax.ppermute(rounded, 'col', [(0, 1), (1, 0)])]
    ppermute x0 -> x2, waiting for transfers between devices: none -> 1.52 us  [the longest x1 1.52 us: shards(): swapped = lax.ppermute(send, 'facet', [(f, f ^ 1) for f in range(facets)])]
    all_to_all x2, starting transfers between devices: 10.9 us -> 9.44 us  [the longest x1 5.91 us: shards(): lax.all_to_all(jnp.broadcast_to(tile_lists, (facets, 1, slots)), 'facet',...]
    slice x1 -> x0, local copies, waits for them, and re-layouts: 1.39 us -> none  [shards(): facet_offsets[0, 0] + first_cell]
    another operation x1 -> x0, other arithmetic: 1.28 us -> none  [shards(): jnp.stack([row_offsets[0], facet_offsets[0, 0] + first_cell, facet_offset...]
    unnamed x4 -> x10, local copies, waits for them, and re-layouts: 1.44 us -> 2.25 us
  transfers between devices with their start and end apart: 2 -> 4, of which waited for: 2 -> 3; matrix products, arithmetic and copies ran while one was open for 0% -> 1% of each run, Pallas kernels for 0% -> 0%
where the time goes in v2:
time: 43.8 us; the launch traced here: 43.2 us
  waiting for transfers between devices  16.6 us (38%)
  starting transfers between devices  12.6 us (29%)
  Pallas kernels  8.36 us (19%)
  local copies, waits for them, and re-layouts  2.85 us (7%)
  between operations  2.03 us (5%)
  other arithmetic  0.79 us (2%)
    all_to_all x1, waiting for transfers between devices, shards(): parts = lax.all_to_all(both, 'facet', 0, 0, tiled=True)  9.33 us
    all_to_all x1, starting transfers between devices, shards(): lax.all_to_all(jnp.broadcast_to(tile_lists, (facets, 1, slots)), 'facet',...  5.91 us
    all_to_all x1, waiting for transfers between devices, shards(): lax.all_to_all(jnp.broadcast_to(tile_lists, (facets, 1, slots)), 'facet',...  5.71 us
    pallas_call x1, Pallas kernels, along(): pl.pallas_call(functools.partial(along_kernel, chunk), out_shape=(jax.Sha...  4.52 us
    all_to_all x1, starting transfers between devices, shards(): parts = lax.all_to_all(both, 'facet', 0, 0, tiled=True)  3.53 us
    ppermute x1, starting transfers between devices, shards(): other = lax.ppermute(rounded, 'col', [(0, 1), (1, 0)])  3.06 us
    unnamed x10, local copies, waits for them, and re-layouts  2.25 us
    pallas_call x1, Pallas kernels, across(): pl.pallas_call(kernel, out_shape=(jax.ShapeDtypeStruct(shape, F32), jax.S...  2.04 us
  transfers between devices with their start and end apart: 4, of which 3 were waited for; matrix products, arithmetic and copies ran while one was open for 1% of the time, Pallas kernels for 0%

profile of v2, /device:TPU:0, one launch (start us, length us, event | category | flops | bytes accessed | tf_op | source)
XLA Modules:
  0.0 43.2 jit_solution(3443872563753550711)
XLA Ops:
  0.0 0.0 copy-start.1
  0.0 0.0 copy-start.4
  0.7 0.0 copy-start
  0.7 0.6 %copy-done = s32[1,2]{1,0:T(1,128)S(1)} copy-done((s32[1,2]{1,0:T(1,128)S(1)}, s32[1,2]{1,0:T(1,128)}, u32[]{:S(2)}) %copy-start) | copy-done | bytes 32
  1.3 0.0 copy-start.2
  1.3 1.6 %copy-done.2 = bf16[1,2,4096,128]{3,2,1,0:T(8,128)(2,1)S(1)} copy-done((bf16[1,2,4096,128]{3,2,1,0:T(8,128)(2,1)S(1)}, bf16[1,2,4096,128]{3,2,1,0:T(8,128)(2,1)}, u32[]{:S(2)}) %copy-start.2) | copy-done | bytes 2097176
  2.9 0.0 copy-start.3
  2.9 4.5 %along.1 = (bf16[256,256]{1,0:T(8,128)(2,1)S(1)}, f32[256,256]{1,0:T(8,128)S(1)}) custom-call(s32[1]{0:T(128)S(6)} %copy.9.rows_at, s32[1,2]{1,0:T(1,128)S(1)} %copy-done, bf16[2,4096,128]{2,1,0:T(8,128)(2,1)S(1)} %bitcast.4), custom_call_target="tpu_custom_call" | custom-call | flops 1073741824 | bytes 2097152 | tf_op jit(solution)/shard_map/along/pallas_call | solution.py:89
  7.5 3.1 %collective-permute-start = (bf16[256,256]{1,0:T(8,128)(2,1)S(1)}, bf16[256,256]{1,0:T(8,128)(2,1)S(1)}, u32[]{:S(2)}, u32[]{:S(2)}) collective-permute-start(bf16[256,256]{1,0:T(8,128)(2,1)S(1)} %get-tuple-element.10), channel_id=1, source_target_pairs={{0,1},{1,0},{2,3},{3,2},{4,5},{5,4},{6,7},{7,6},{8,9},{9,8},{10,11... | collective-permute-start | bytes 393224 | tf_op jit(solution)/shard_map/ppermute | solution.py:259
  10.5 0.0 copy-done.4
  10.5 0.6 %broadcast_in_dim.11 = s32[16,1,8]{2,1,0:T(1,128)} broadcast(s32[8]{0:T(128)S(1)} %bitcast.6), dimensions={2} | broadcast | bytes 544 | tf_op jit(solution)/shard_map/broadcast_in_dim | solution.py:254
  11.1 5.9 %all-to-all-start = ((s32[16,1,8]{2,1,0:T(1,128)}), s32[16,1,8]{2,1,0:T(1,128)S(1)}, u32[]{:S(2)}, u32[]{:S(2)}) async-start(s32[16,1,8]{2,1,0:T(1,128)} %broadcast_in_dim.11), calls=%async_computation | async-start | bytes 16384 | tf_op jit(solution)/shard_map/all_to_all | solution.py:253
  17.7 5.7 %all-to-all-done.names = s32[16,1,8]{2,1,0:T(1,128)S(1)} async-done(((s32[16,1,8]{2,1,0:T(1,128)}), s32[16,1,8]{2,1,0:T(1,128)S(1)}, u32[]{:S(2)}, u32[]{:S(2)}) %all-to-all-start) | async-done | bytes 544 | tf_op jit(solution)/shard_map/all_to_all | solution.py:253
  23.4 0.0 collective-permute-done.other
  23.4 0.0 copy-done.1
  23.4 2.0 %across.1 = (f32[16,2,32,128]{3,2,1,0:T(8,128)S(1)}, bf16[16,2,32,128]{3,2,1,0:T(8,128)(2,1)S(1)}) custom-call(s32[1]{0:T(128)S(6)} %copy.8.columns, s32[1,2]{1,0:T(1,128)S(1)} %copy-done.1, s32[16,1,8]{2,1,0:T(1,128)S(1)} %all-to-all-done.names, f32[256,256]{1,0:T(8,128)S(1)} %get-tuple-element.9.own, bf16[256,256]{1,0:T(8,128)(2,1)S(1)} %collective-permute-done.other), custom_call_target="tpu_custom_call" | custom-call | flops 67108864 | bytes 1048576 | tf_op jit(solution)/shard_map/across/pallas_call | solution.py:164
  25.5 0.1 collective-permute-start.1
  25.5 1.5 %collective-permute-done.1 = bf16[16,2,32,128]{3,2,1,0:T(8,128)(2,1)S(1)} collective-permute-done((bf16[16,2,32,128]{3,2,1,0:T(8,128)(2,1)S(1)}, bf16[16,2,32,128]{3,2,1,0:T(8,128)(2,1)S(1)}, u32[]{:S(2)}, u32[]{:S(2)}) %collective-permute-start.1) | collective-permute-done | bytes 262176 | tf_op jit(solution)/shard_map/ppermute | solution.py:263
  27.1 0.8 %add_convert_fusion = bf16[16,2,32,128]{3,2,1,0:T(8,128)(2,1)} fusion(f32[16,2,32,128]{3,2,1,0:T(8,128)S(1)} %get-tuple-element.11, bf16[16,2,32,128]{3,2,1,0:T(8,128)(2,1)S(1)} %collective-permute-done.1), kind=kLoop, calls=%fused_computation | loop fusion | flops 393216 | bytes 1048576 | tf_op jit(solution)/shard_map/convert_element_type | solution.py:264
  27.8 3.5 %all-to-all-start.1 = ((bf16[16,2,32,128]{3,2,1,0:T(8,128)(2,1)}), bf16[16,2,32,128]{3,2,1,0:T(8,128)(2,1)S(1)}, u32[]{:S(2)}, u32[]{:S(2)}) async-start(bf16[16,2,32,128]{3,2,1,0:T(8,128)(2,1)} %add_convert_fusion), calls=%async_computation.1 | async-start | bytes 524288 | tf_op jit(solution)/shard_map/all_to_all | solution.py:265
  32.0 9.3 %all-to-all-done.1.parts = bf16[16,2,32,128]{3,2,1,0:T(8,128)(2,1)S(1)} async-done(((bf16[16,2,32,128]{3,2,1,0:T(8,128)(2,1)}), bf16[16,2,32,128]{3,2,1,0:T(8,128)(2,1)S(1)}, u32[]{:S(2)}, u32[]{:S(2)}) %all-to-all-start.1) | async-done | bytes 262176 | tf_op jit(solution)/shard_map/all_to_all | solution.py:265
  41.4 0.0 copy-done.3
  41.4 1.8 %visibility.1 = f32[8,2,1024]{2,1,0:T(2,128)} custom-call(s32[1,1]{1,0:T(1,128)S(6)} %copy.10.live, bf16[16,2,32,128]{3,2,1,0:T(8,128)(2,1)S(1)} %all-to-all-done.1.parts, s32[8,2,1024]{2,1,0:T(2,128)S(1)} %bitcast.5), custom_call_target="tpu_custom_call" | custom-call | flops 134217728 | bytes 1048576 | tf_op jit(solution)/shard_map/visibility/pallas_call | solution.py:227
Async XLA Ops:
  0.0 23.4 %copy-start.1 = (s32[1,2]{1,0:T(1,128)S(1)}, s32[1,2]{1,0:T(1,128)}, u32[]{:S(2)}) copy-start(s32[1,2]{1,0:T(1,128)} %offsets.3) | copy-start | bytes 28
  0.0 10.5 %copy-start.4 = (s32[1,1,8]{2,1,0:T(1,128)S(1)}, s32[1,1,8]{2,1,0:T(1,128)}, u32[]{:S(2)}) copy-start(s32[1,1,8]{2,1,0:T(1,128)} %param.11) | copy-start | bytes 100
  0.7 0.7 %copy-start = (s32[1,2]{1,0:T(1,128)S(1)}, s32[1,2]{1,0:T(1,128)}, u32[]{:S(2)}) copy-start(s32[1,2]{1,0:T(1,128)} %offsets.3) | copy-start | bytes 28
  1.3 1.6 %copy-start.2 = (bf16[1,2,4096,128]{3,2,1,0:T(8,128)(2,1)S(1)}, bf16[1,2,4096,128]{3,2,1,0:T(8,128)(2,1)}, u32[]{:S(2)}) copy-start(bf16[1,2,4096,128]{3,2,1,0:T(8,128)(2,1)} %param.7) | copy-start | bytes 6291460
  2.9 38.4 %copy-start.3 = (s32[1,1,8,2,1024]{4,3,2,1,0:T(2,128)S(1)}, s32[1,1,8,2,1024]{4,3,2,1,0:T(2,128)}, u32[]{:S(2)}) copy-start(s32[1,1,8,2,1024]{4,3,2,1,0:T(2,128)} %param.13) | copy-start | bytes 196612
  7.5 15.9 %collective-permute-start = (bf16[256,256]{1,0:T(8,128)(2,1)S(1)}, bf16[256,256]{1,0:T(8,128)(2,1)S(1)}, u32[]{:S(2)}, u32[]{:S(2)}) collective-permute-start(bf16[256,256]{1,0:T(8,128)(2,1)S(1)} %get-tuple-element.10), channel_id=1, source_target_pairs={{0,1},{1,0},{2,3},{3,2},{4,5},{5,4},{6,7},{7,6},{8,9},{9,8},{10,11... | collective-permute-start | bytes 393224 | tf_op jit(solution)/shard_map/ppermute | solution.py:259
  11.1 12.3 %all-to-all-start = ((s32[16,1,8]{2,1,0:T(1,128)}), s32[16,1,8]{2,1,0:T(1,128)S(1)}, u32[]{:S(2)}, u32[]{:S(2)}) async-start(s32[16,1,8]{2,1,0:T(1,128)} %broadcast_in_dim.11), calls=%async_computation | async-start | bytes 16384 | tf_op jit(solution)/shard_map/all_to_all | solution.py:253
  25.5 1.6 %collective-permute-start.1 = (bf16[16,2,32,128]{3,2,1,0:T(8,128)(2,1)S(1)}, bf16[16,2,32,128]{3,2,1,0:T(8,128)(2,1)S(1)}, u32[]{:S(2)}, u32[]{:S(2)}) collective-permute-start(bf16[16,2,32,128]{3,2,1,0:T(8,128)(2,1)S(1)} %get-tuple-element.12), channel_id=1, source_target_pairs={{0,2},{2,0},{4,6},{6,4},{8,10},{10,8},{12,14},{14,12},{16,18},{18,... | collective-permute-start | bytes 786440 | tf_op jit(solution)/shard_map/ppermute | solution.py:263
  27.8 13.5 %all-to-all-start.1 = ((bf16[16,2,32,128]{3,2,1,0:T(8,128)(2,1)}), bf16[16,2,32,128]{3,2,1,0:T(8,128)(2,1)S(1)}, u32[]{:S(2)}, u32[]{:S(2)}) async-start(bf16[16,2,32,128]{3,2,1,0:T(8,128)(2,1)} %add_convert_fusion), calls=%async_computation.1 | async-start | bytes 524288 | tf_op jit(solution)/shard_map/all_to_all | solution.py:265

commit v3 on v1

v3 whole, which is shorter than its diff:
```python
import functools
import math

import jax
import jax.numpy as jnp
from jax import lax
from jax.experimental import pallas as pl
from jax.experimental.pallas import tpu as pltpu
from jax.sharding import PartitionSpec as P


L = 8192
W = 128
S = 256
TILE = 32
NTOT = 65536
UV_STEPS = 4096
VMEM_LIMIT = 16 << 20
BF16 = jnp.bfloat16
F32 = jnp.float32
I32 = jnp.int32


def cos_sin(index):
    shifted = index + NTOT // 8
    quadrant = shifted >> 14
    rest = (shifted & (NTOT // 4 - 1)) - NTOT // 8
    x = rest.astype(F32) * (2.0 * math.pi / NTOT)
    y = x * x
    sine = x + x * (y * (-1.0 / 6 + y * (1.0 / 120 + y * (-1.0 / 5040 + y * (1.0 / 362880)))))
    cosine = 1.0 + y * (-0.5 + y * (1.0 / 24 + y * (-1.0 / 720 + y * (1.0 / 40320))))
    odd = (quadrant & 1) != 0
    first = jnp.where(odd, sine, cosine)
    second = jnp.where(odd, cosine, sine)
    return (
        jnp.where(((quadrant + 1) & 2) != 0, -first, first),
        jnp.where((quadrant & 2) != 0, -second, second),
    )


def mod_phase(first, second):
    return (first * second) & (NTOT - 1)


def split(facets):
    groups = max(1, facets // TILE)
    inside = TILE * groups // facets
    return groups, S // TILE // groups, inside


def along_kernel(facets, cols, chunk, scal, offsets, names, strip, out, held, table, total, small, sems):
    count = held.shape[1]
    steps = count // chunk
    slots = names.shape[2]
    copies = []
    notes = []
    for n, (src, dst) in enumerate(zip((offsets, names), small)):
        notes.append(pltpu.make_async_copy(src, dst, sems.at[steps + n]))
        notes[n].start()
    for n in range(steps):
        part = pl.ds(n * chunk, chunk)
        copies.append(pltpu.make_async_copy(strip.at[:, part], held.at[:, part], sems.at[n]))
        copies[n].start()
    for copy in notes:
        copy.wait()
    row_start = scal[0]
    col_start = small[0][0, 0] + lax.axis_index("col") * count
    rows = S // facets
    groups, tall, inside = split(facets)
    place = lax.broadcasted_iota(I32, (S, W), 0)
    lane = lax.broadcasted_iota(I32, (S, W), 1)
    owner = place // rows
    within = place % rows
    sample = (
        (within % tall + tall * (owner // (facets // groups))) * TILE
        + (owner % (facets // groups)) * inside
        + within // tall
    )
    row = row_start + (NTOT // L) * sample
    cos_in, sin_in = cos_sin(mod_phase(row, lane))
    cos_out, sin_out = cos_sin(mod_phase(row, col_start + W * lane))
    scale = 1.0 / math.sqrt(L)
    cos_out = cos_out * scale
    sin_out = sin_out * scale
    for n in range(steps):
        for local in range(chunk // W):
            a = n * (chunk // W) + local
            c = cos_out[:, a : a + 1]
            s = sin_out[:, a : a + 1]
            at = slice(local * W, (local + 1) * W)
            table[n % 2, 0:S, at] = (c * cos_in - s * sin_in).astype(BF16)
            table[n % 2, S : 2 * S, at] = (s * cos_in + c * sin_in).astype(BF16)
        copies[n].wait()
        part = slice(n * chunk, (n + 1) * chunk)
        cells = jnp.concatenate([held[0, part, :], held[1, part, :]], axis=1)
        term = jnp.dot(table[n % 2], cells, preferred_element_type=F32)
        if n == 0:
            total[...] = term
        else:
            total[...] += term
    real = total[0:S, 0:W] + total[S : 2 * S, W : 2 * W]
    imag = total[0:S, W : 2 * W] - total[S : 2 * S, 0:W]
    total[0:S, 0:W] = real
    total[0:S, W : 2 * W] = imag
    across = small[0][0, 1]
    line = lax.broadcasted_iota(I32, (slots, W), 0)
    spot = lax.broadcasted_iota(I32, (slots, W), 1)
    note = jnp.zeros((slots, W), I32)
    for j in range(slots):
        note = jnp.where(line == j, small[1][0, 0, j], note)
    note = jnp.where(spot == W - 2, across >> 8, jnp.where(spot == W - 1, across & 255, note))
    note = note.astype(F32).astype(BF16)
    for o in range(facets):
        re = total[o * rows : (o + 1) * rows, 0:W].astype(BF16)
        im = total[o * rows : (o + 1) * rows, W : 2 * W].astype(BF16)
        for c in range(cols):
            out[o * cols + c, 0:rows, :] = re
            out[o * cols + c, rows : 2 * rows, :] = im
            out[o * cols + c, 2 * rows :, :] = note


def along(strip, row_offsets, facet_offsets, names, facets, cols):
    count = strip.shape[1]
    chunk = min(1024, count)
    rows = S // facets
    slots = names.shape[2]
    return pl.pallas_call(
        functools.partial(along_kernel, facets, cols, chunk),
        out_shape=jax.ShapeDtypeStruct((facets * cols, 2 * rows + slots, W), BF16),
        in_specs=[pl.BlockSpec(memory_space=pltpu.SMEM)]
        + [pl.BlockSpec(memory_space=pltpu.HBM)] * 3,
        out_specs=pl.BlockSpec(memory_space=pltpu.VMEM),
        scratch_shapes=[
            pltpu.VMEM((2, count, W), BF16),
            pltpu.VMEM((2, 2 * S, chunk), BF16),
            pltpu.VMEM((2 * S, 2 * W), F32),
            [
                pltpu.SMEM(facet_offsets.shape, I32),
                pltpu.SMEM(names.shape, I32),
            ],
            pltpu.SemaphoreType.DMA((count // chunk + 2,)),
        ],
        cost_estimate=pl.CostEstimate(
            flops=8 * S * W * count, bytes_accessed=4 * count * W, transcendentals=0
        ),
        name="along",
    )(row_offsets, facet_offsets, names, strip)


def base_kernel(columns, out):
    cell = lax.broadcasted_iota(I32, (W, 2 * S), 0)
    lane = lax.broadcasted_iota(I32, (W, 2 * S), 1)
    turn = ((lane >> 5) & 1) * (NTOT // 4)
    top, bottom = cos_sin((cell * positions(columns[0], lane) + turn) & (NTOT - 1))
    scale = 1.0 / math.sqrt(W)
    out[0:W, :] = (top * scale).astype(BF16)
    out[W : 2 * W, :] = (bottom * scale).astype(BF16)


def positions(column, lane):
    return column + (NTOT // S) * ((lane >> 6) * TILE + (lane & (TILE - 1)))


def base(columns):
    return pl.pallas_call(
        base_kernel,
        out_shape=jax.ShapeDtypeStruct((2 * W, 2 * S), BF16),
        in_specs=[pl.BlockSpec(memory_space=pltpu.SMEM)],
        out_specs=pl.BlockSpec(memory_space=pltpu.VMEM),
        compiler_params=pltpu.CompilerParams(vmem_limit_bytes=VMEM_LIMIT),
        cost_estimate=pl.CostEstimate(flops=1 << 24, bytes_accessed=1 << 18, transcendentals=0),
        name="base",
    )(columns)


def across_kernel(facets, cols, columns, got, right, out, left, summed, phases):
    rows = S // facets
    groups, tall, inside = split(facets)
    slots = got.shape[1] - 2 * rows
    wide = 2 * S
    height = facets * rows
    column = lax.axis_index("col")
    sources = []
    for f in range(facets):
        re = got[f * cols, 0:rows, :].astype(F32)
        im = got[f * cols, rows : 2 * rows, :].astype(F32)
        for h in range(1, cols):
            re = re + got[f * cols + h, 0:rows, :].astype(F32)
            im = im + got[f * cols + h, rows : 2 * rows, :].astype(F32)
        left[f * rows : (f + 1) * rows, 0:W] = re
        left[f * rows : (f + 1) * rows, W : 2 * W] = im
        left[height + f * rows : height + (f + 1) * rows, 0:W] = im
        left[height + f * rows : height + (f + 1) * rows, W : 2 * W] = -re
        sources.append(got[f * cols + column, 2 * rows :, :].astype(F32))
    summed[...] = jnp.dot(left[...].astype(BF16), right[...], preferred_element_type=F32)
    heads = jnp.concatenate([note[0:1] for note in sources], axis=0)
    offset = (heads[:, W - 2 : W - 1] * 256.0 + heads[:, W - 1 : W]).astype(I32)
    lane = lax.broadcasted_iota(I32, (facets, wide), 1)
    cosine, sine = cos_sin(mod_phase(offset, positions(columns[0], lane)))
    phases[0] = cosine
    phases[1] = sine
    acc = jnp.zeros((rows, wide), F32)
    for f in range(facets):
        acc = acc + summed[f * rows : (f + 1) * rows, :] * phases[0, f : f + 1, :]
        acc = acc + summed[height + f * rows : height + (f + 1) * rows, :] * phases[1, f : f + 1, :]
    acc = acc * (1.0 / math.sqrt(facets))
    pieces = []
    for b in range(S // TILE):
        at = slice(b * 2 * TILE, (b + 1) * 2 * TILE)
        parts = [acc[i * tall : (i + 1) * tall, at] for i in range(inside)]
        if inside == 1:
            parts.append(jnp.zeros_like(parts[0]))
        pieces.append(jnp.concatenate(parts, axis=1))
    tiles = jnp.concatenate(pieces, axis=0).astype(BF16)
    names = jnp.concatenate(sources, axis=0).astype(I32)
    first = (lax.axis_index("facet") // (facets // groups)) * tall
    local = (names >> 3) - first
    wanted = jnp.where((local >= 0) & (local < tall), (names & 7) * tall + local, -1)
    count = tiles.shape[0]
    spot = lax.broadcasted_iota(I32, (facets * slots, W), 1)
    onehot = jnp.where(wanted == spot, 1.0, 0.0).astype(BF16)[:, 0:count]
    chosen = jnp.dot(onehot, tiles, preferred_element_type=F32)
    for o in range(facets):
        out[o] = chosen[o * slots : (o + 1) * slots, :].astype(BF16)


def across(got, right, columns, facets, cols):
    rows = S // facets
    slots = got.shape[1] - 2 * rows
    return pl.pallas_call(
        functools.partial(across_kernel, facets, cols),
        out_shape=jax.ShapeDtypeStruct((facets, slots, W), BF16),
        in_specs=[
            pl.BlockSpec(memory_space=pltpu.SMEM),
            pl.BlockSpec(memory_space=pltpu.VMEM),
            pl.BlockSpec(memory_space=pltpu.VMEM),
        ],
        out_specs=pl.BlockSpec(memory_space=pltpu.VMEM),
        scratch_shapes=[
            pltpu.VMEM((2 * S, 2 * W), F32),
            pltpu.VMEM((2 * S, 2 * S), F32),
            pltpu.VMEM((2, facets, 2 * S), F32),
        ],
        compiler_params=pltpu.CompilerParams(vmem_limit_bytes=VMEM_LIMIT),
        cost_estimate=pl.CostEstimate(
            flops=2 * 2 * S * 2 * W * 2 * S, bytes_accessed=1 << 20, transcendentals=0
        ),
        name="across",
    )(columns, got, right)


def waves_kernel(facets, uv, right, near, far):
    _, _, inside = split(facets)
    vis = uv.shape[2]
    step = NTOT // UV_STEPS
    line = lax.broadcasted_iota(I32, (TILE, vis), 0)
    low = line[0:8] * inside
    high = (line[0:4] % (4 // inside)) * 8 * inside + line[0:4] // (4 // inside)

    def slot(j, carry):
        cosine, sine = cos_sin((uv[j, 1:2, :] * (line * step)) & (NTOT - 1))
        cos_high, sin_high = cosine.astype(BF16), sine.astype(BF16)
        right[j, 0:TILE, :] = cos_high
        right[j, TILE : 2 * TILE, :] = sin_high
        right[j, 2 * TILE : 3 * TILE, :] = (cosine - cos_high.astype(F32)).astype(BF16)
        right[j, 3 * TILE : 4 * TILE, :] = (sine - sin_high.astype(F32)).astype(BF16)
        cosine, sine = cos_sin((uv[j, 0:1, :] * (low * step)) & (NTOT - 1))
        near[j, 0] = cosine * (1.0 / TILE)
        near[j, 1] = sine * (1.0 / TILE)
        cosine, sine = cos_sin((uv[j, 0:1, :] * (high * step)) & (NTOT - 1))
        far[j, 0] = cosine
        far[j, 1] = sine
        return carry

    lax.fori_loop(0, uv.shape[0], slot, 0)


def waves(uv, facets):
    slots, _, vis = uv.shape
    return pl.pallas_call(
        functools.partial(waves_kernel, facets),
        out_shape=(
            jax.ShapeDtypeStruct((slots, 4 * TILE, vis), BF16),
            jax.ShapeDtypeStruct((slots, 2, 8, vis), F32),
            jax.ShapeDtypeStruct((slots, 2, 4, vis), F32),
        ),
        in_specs=[pl.BlockSpec(memory_space=pltpu.VMEM)],
        out_specs=[pl.BlockSpec(memory_space=pltpu.VMEM)] * 3,
        compiler_params=pltpu.CompilerParams(vmem_limit_bytes=VMEM_LIMIT),
        cost_estimate=pl.CostEstimate(flops=1 << 26, bytes_accessed=3 << 20, transcendentals=0),
        name="waves",
    )(uv)


def visibility_kernel(facets, live, parts, right, near, far, out, held):
    groups, _, inside = split(facets)
    slots, vis = out.shape[0], out.shape[2]
    sources = facets // groups
    for f in range(sources):
        held[f] = parts[f].astype(F32)
        for g in range(1, groups):
            held[f] += parts[g * sources + f].astype(F32)
    lane = lax.broadcasted_iota(I32, (sources, W), 1)
    sign = jnp.where((lane & TILE) == 0, 1.0, -1.0).astype(F32)
    for j in range(slots):
        @pl.when(j < live[0, 0])
        def _():
            x = held[:, j, :]
            y = pltpu.roll(x, W // 2, 1)
            both = [jnp.where(lane < W // 2, x, y), jnp.where(lane < W // 2, y, x)][:inside]
            lhs = [z * sign for z in both] + [pltpu.roll(z, TILE, 1) for z in both]
            middle = jnp.dot(
                jnp.concatenate(lhs, axis=0).astype(BF16), right[j], preferred_element_type=F32
            )
            real, imag = middle[0:8], middle[TILE : TILE + 8]
            for h in range(1, 4):
                more_re = middle[8 * h : 8 * h + 8]
                more_im = middle[TILE + 8 * h : TILE + 8 * h + 8]
                cosine, sine = far[j, 0, h : h + 1, :], far[j, 1, h : h + 1, :]
                real = real + (cosine * more_re - sine * more_im)
                imag = imag + (cosine * more_im + sine * more_re)
            cosine, sine = near[j, 0], near[j, 1]
            out[j, 0:1, :] = jnp.sum(cosine * real - sine * imag, axis=0, keepdims=True)
            out[j, 1:2, :] = jnp.sum(cosine * imag + sine * real, axis=0, keepdims=True)

        @pl.when(j >= live[0, 0])
        def _():
            out[j] = jnp.zeros((2, vis), F32)


def visibilities_of(parts, live, tables, facets):
    slots, _, vis = tables[0].shape
    return pl.pallas_call(
        functools.partial(visibility_kernel, facets),
        out_shape=jax.ShapeDtypeStruct((slots, 2, vis), F32),
        in_specs=[pl.BlockSpec(memory_space=pltpu.SMEM)]
        + [pl.BlockSpec(memory_space=pltpu.VMEM)] * 4,
        out_specs=pl.BlockSpec(memory_space=pltpu.VMEM),
        scratch_shapes=[pltpu.VMEM((facets // split(facets)[0], slots, W), F32)],
        compiler_params=pltpu.CompilerParams(vmem_limit_bytes=VMEM_LIMIT),
        cost_estimate=pl.CostEstimate(
            flops=slots * 2 * 64 * 128 * vis, bytes_accessed=1 << 20, transcendentals=0
        ),
        name="visibility",
    )(live, parts, *tables)


def shards(
    facet_strips, facet_offsets, column_offsets, row_offsets, tile_lists, tile_counts, uv_index
):
    facets, cols = lax.axis_size("facet"), lax.axis_size("col")
    sent = along(facet_strips[0], row_offsets, facet_offsets, tile_lists, facets, cols)
    got = lax.all_to_all(sent, ("facet", "col"), 0, 0, tiled=True)
    right = base(column_offsets)
    asked = across(got, right, column_offsets, facets, cols)
    parts = lax.all_to_all(asked, "facet", 0, 0, tiled=True)
    tables = waves(uv_index[0, 0], facets)
    result = visibilities_of(parts, tile_counts, tables, facets)
    return result[None, None]


def solution(mesh):
    in_specs = (
        P("facet", None, "col", None),
        P("facet", None),
        P("col"),
        P(),
        P("col", "facet", None),
        P("col", "facet"),
        P("col", "facet", None, None, None),
    )
    out_specs = P("col", "facet", None, None, None)
    return jax.shard_map(shards, mesh=mesh, in_specs=in_specs, out_specs=out_specs, check_vma=False)
```

time: 50.8 us -> 38 us (0.75); the launches traced: 51.4 us -> 37.7 us
  waiting for transfers between devices: 20.4 us -> 14.1 us
  local copies, waits for them, and re-layouts: 2.83 us -> 0.01 us
  Pallas kernels: 13.4 us -> 10.8 us
  other arithmetic: 1.28 us -> 0 us
  between operations: 2.62 us -> 2 us
    all_to_all x2, waiting for transfers between devices: 20.4 us -> 14.1 us  [the longest x1 10.6 us: shards(): got = lax.all_to_all(sent, ('facet', 'col'), 0, 0, tiled=True)]
    pallas_call x1, Pallas kernels: 5.45 us -> 1.37 us  [visibilities_of(): pl.pallas_call(functools.partial(visibility_kernel, facets), out_shape=ja...]
    pallas_call x0 -> x2, Pallas kernels: none -> 2.84 us  [the longest x1 2.43 us: waves(): pl.pallas_call(functools.partial(waves_kernel, facets), out_shape=(jax.Sh...]
    pallas_call x1, Pallas kernels: 2.66 us -> 1.12 us  [across(): pl.pallas_call(functools.partial(across_kernel, facets, cols), out_shape=...]
    unnamed x4 -> x2, local copies, waits for them, and re-layouts: 1.44 us -> 0.01 us
    slice x1 -> x0, local copies, waits for them, and re-layouts: 1.39 us -> none  [shards(): facet_offsets[0, 0] + first_cell]
    another operation x1 -> x0, other arithmetic: 1.28 us -> none  [shards(): jnp.stack([row_offsets[0], facet_offsets[0, 0] + first_cell, facet_offset...]
  transfers between devices with their start and end apart: 2 -> 2, of which waited for: 2 -> 2; matrix products, arithmetic and copies ran while one was open for 0% -> 0% of each run, Pallas kernels for 0% -> 8%
where the time goes in v3:
time: 38 us; the launch traced here: 37.7 us
  waiting for transfers between devices  14.1 us (37%)
  Pallas kernels  10.8 us (28%)
  starting transfers between devices  10.8 us (28%)
  between operations  2 us (5%)
    all_to_all x1, waiting for transfers between devices, shards(): got = lax.all_to_all(sent, ('facet', 'col'), 0, 0, tiled=True)  10.6 us
    all_to_all x1, starting transfers between devices, shards(): got = lax.all_to_all(sent, ('facet', 'col'), 0, 0, tiled=True)  7.33 us
    pallas_call x1, Pallas kernels, along(): pl.pallas_call(functools.partial(along_kernel, facets, cols, chunk), out_...  5.43 us
    all_to_all x1, waiting for transfers between devices, shards(): parts = lax.all_to_all(asked, 'facet', 0, 0, tiled=True)  3.51 us
    all_to_all x1, starting transfers between devices, shards(): parts = lax.all_to_all(asked, 'facet', 0, 0, tiled=True)  3.5 us
    pallas_call x1, Pallas kernels, waves(): pl.pallas_call(functools.partial(waves_kernel, facets), out_shape=(jax.Sh...  2.43 us
    pallas_call x1, Pallas kernels, visibilities_of(): pl.pallas_call(functools.partial(visibility_kernel, facets), out_shape=ja...  1.37 us
    pallas_call x1, Pallas kernels, across(): pl.pallas_call(functools.partial(across_kernel, facets, cols), out_shape=...  1.12 us
  transfers between devices with their start and end apart: 2, of which 2 were waited for; matrix products, arithmetic and copies ran while one was open for 0% of the time, Pallas kernels for 8%

profile of v3, /device:TPU:0, one launch (start us, length us, event | category | flops | bytes accessed | tf_op | source)
XLA Modules:
  0.0 37.7 jit_solution(7804347048391486506)
XLA Ops:
  0.7 0.0 copy-start
  0.7 5.4 %along.1 = bf16[32,40,128]{2,1,0:T(8,128)(2,1)} custom-call(s32[1]{0:T(128)S(6)} %copy.9.scal, s32[1,2]{1,0:T(1,128)} %offsets.1, s32[1,1,8]{2,1,0:T(1,128)} %names.1, bf16[2,4096,128]{2,1,0:T(8,128)(2,1)} %bitcast.4), custom_call_target="tpu_custom_call" | custom-call | flops 1073741824 | bytes 2097152 | tf_op jit(solution)/shard_map/along/pallas_call | solution.py:127
  6.1 7.3 %all-to-all-start = ((bf16[32,40,128]{2,1,0:T(8,128)(2,1)}), bf16[32,40,128]{2,1,0:T(8,128)(2,1)S(1)}, u32[]{:S(2)}, u32[]{:S(2)}) async-start(bf16[32,40,128]{2,1,0:T(8,128)(2,1)} %along.1), calls=%async_computation | async-start | bytes 655360 | tf_op jit(solution)/shard_map/all_to_all | solution.py:353
  14.1 0.4 %base.1.right = bf16[256,512]{1,0:T(8,128)(2,1)S(1)} custom-call(s32[1]{0:T(128)S(6)} %copy.8.columns), custom_call_target="tpu_custom_call" | custom-call | flops 16777216 | bytes 262144 | tf_op jit(solution)/shard_map/base/pallas_call | solution.py:165
  14.5 10.6 %all-to-all-done.got = bf16[32,40,128]{2,1,0:T(8,128)(2,1)S(1)} async-done(((bf16[32,40,128]{2,1,0:T(8,128)(2,1)}), bf16[32,40,128]{2,1,0:T(8,128)(2,1)S(1)}, u32[]{:S(2)}, u32[]{:S(2)}) %all-to-all-start) | async-done | bytes 327712 | tf_op jit(solution)/shard_map/all_to_all | solution.py:353
  25.1 1.1 %across.1 = bf16[16,8,128]{2,1,0:T(8,128)(2,1)} custom-call(s32[1]{0:T(128)S(6)} %copy.8.columns, bf16[32,40,128]{2,1,0:T(8,128)(2,1)S(1)} %all-to-all-done.got, bf16[256,512]{1,0:T(8,128)(2,1)S(1)} %base.1.right), custom_call_target="tpu_custom_call" | custom-call | flops 134217728 | bytes 1048576 | tf_op jit(solution)/shard_map/across/pallas_call | solution.py:230
  26.3 3.5 %all-to-all-start.1 = ((bf16[16,8,128]{2,1,0:T(8,128)(2,1)}), bf16[16,8,128]{2,1,0:T(8,128)(2,1)S(1)}, u32[]{:S(2)}, u32[]{:S(2)}) async-start(bf16[16,8,128]{2,1,0:T(8,128)(2,1)} %across.1), calls=%async_computation.1 | async-start | bytes 65536 | tf_op jit(solution)/shard_map/all_to_all | solution.py:356
  30.4 0.0 copy-done
  30.4 2.4 %waves.1 = (bf16[8,128,1024]{2,1,0:T(8,128)(2,1)S(1)}, f32[8,2,8,1024]{3,2,1,0:T(8,128)S(1)}, f32[8,2,4,1024]{3,2,1,0:T(4,128)S(1)}) custom-call(s32[8,2,1024]{2,1,0:T(2,128)S(1)} %bitcast.3), custom_call_target="tpu_custom_call" | custom-call | flops 67108864 | bytes 3145728 | tf_op jit(solution)/shard_map/waves/pallas_call | solution.py:280
  32.8 3.5 %all-to-all-done.1.parts = bf16[16,8,128]{2,1,0:T(8,128)(2,1)S(1)} async-done(((bf16[16,8,128]{2,1,0:T(8,128)(2,1)}), bf16[16,8,128]{2,1,0:T(8,128)(2,1)S(1)}, u32[]{:S(2)}, u32[]{:S(2)}) %all-to-all-start.1) | async-done | bytes 32800 | tf_op jit(solution)/shard_map/all_to_all | solution.py:356
  36.4 1.4 %visibility.1 = f32[8,2,1024]{2,1,0:T(2,128)} custom-call(s32[1,1]{1,0:T(1,128)S(6)} %copy.10.live, bf16[16,8,128]{2,1,0:T(8,128)(2,1)S(1)} %all-to-all-done.1.parts, bf16[8,128,1024]{2,1,0:T(8,128)(2,1)S(1)} %get-tuple-element.8.right, f32[8,2,8,1024]{3,2,1,0:T(8,128)S(1)} %get-tuple-element.9.near, f32[8,2,4,1024]{3,2,1,0:T(4,128)S(1)} %get-tuple-element.10.far), custom_call_target="tpu_custom_call" | custom-call | flops 134217728 | bytes 1048576 | tf_op jit(solution)/shard_map/visibility/pallas_call | solution.py:333
Async XLA Ops:
  0.7 29.8 %copy-start = (s32[1,1,8,2,1024]{4,3,2,1,0:T(2,128)S(1)}, s32[1,1,8,2,1024]{4,3,2,1,0:T(2,128)}, u32[]{:S(2)}) copy-start(s32[1,1,8,2,1024]{4,3,2,1,0:T(2,128)} %param.13) | copy-start | bytes 196612
  6.1 19.0 %all-to-all-start = ((bf16[32,40,128]{2,1,0:T(8,128)(2,1)}), bf16[32,40,128]{2,1,0:T(8,128)(2,1)S(1)}, u32[]{:S(2)}, u32[]{:S(2)}) async-start(bf16[32,40,128]{2,1,0:T(8,128)(2,1)} %along.1), calls=%async_computation | async-start | bytes 655360 | tf_op jit(solution)/shard_map/all_to_all | solution.py:353
  26.3 10.1 %all-to-all-start.1 = ((bf16[16,8,128]{2,1,0:T(8,128)(2,1)}), bf16[16,8,128]{2,1,0:T(8,128)(2,1)S(1)}, u32[]{:S(2)}, u32[]{:S(2)}) async-start(bf16[16,8,128]{2,1,0:T(8,128)(2,1)} %across.1), calls=%async_computation.1 | async-start | bytes 65536 | tf_op jit(solution)/shard_map/all_to_all | solution.py:356

commit v4 on v3

--- a/solution.py
+++ b/solution.py
@@ -16,6 +16,8 @@
 NTOT = 65536
 UV_STEPS = 4096
 VMEM_LIMIT = 16 << 20
+CHUNK = 512
+CHAIN = 16
 BF16 = jnp.bfloat16
 F32 = jnp.float32
 I32 = jnp.int32
@@ -48,7 +50,7 @@
     return groups, S // TILE // groups, inside
 
 
-def along_kernel(facets, cols, chunk, scal, offsets, names, strip, out, held, table, total, small, sems):
+def along_kernel(facets, cols, chunk, scal, offsets, names, strip, out, held, table, total, state, outside, small, sems):
     count = held.shape[1]
     steps = count // chunk
     slots = names.shape[2]
@@ -67,30 +69,74 @@
     col_start = small[0][0, 0] + lax.axis_index("col") * count
     rows = S // facets
     groups, tall, inside = split(facets)
-    place = lax.broadcasted_iota(I32, (S, W), 0)
-    lane = lax.broadcasted_iota(I32, (S, W), 1)
-    owner = place // rows
-    within = place % rows
-    sample = (
-        (within % tall + tall * (owner // (facets // groups))) * TILE
-        + (owner % (facets // groups)) * inside
-        + within // tall
-    )
-    row = row_start + (NTOT // L) * sample
-    cos_in, sin_in = cos_sin(mod_phase(row, lane))
-    cos_out, sin_out = cos_sin(mod_phase(row, col_start + W * lane))
-    scale = 1.0 / math.sqrt(L)
-    cos_out = cos_out * scale
-    sin_out = sin_out * scale
+
+    def sample_of(place):
+        owner = place // rows
+        within = place % rows
+        group = owner // (facets // groups)
+        line = (owner % (facets // groups)) * inside + within // tall
+        return (within % tall + tall * group) * TILE + line
+
+    blocks = S // 8
+    inner = row_start + (NTOT // L) * sample_of(lax.broadcasted_iota(I32, (8, W), 0))
+    outer = (NTOT // L) * sample_of(8 * lax.broadcasted_iota(I32, (blocks, W), 0))
+    cell = col_start + lax.broadcasted_iota(I32, (8, W), 1)
+    cells_of = {"first": (cell, 1.0 / math.sqrt(L)), "step": (W, 1.0), "leap": (CHAIN * W, 1.0)}
+    factors = []
+    for n, (column, scale) in enumerate(cells_of.values()):
+        cosine, sine = cos_sin(mod_phase(inner, column))
+        factors.append((cosine * scale, sine * scale))
+        if n == 0:
+            column = col_start + lax.broadcasted_iota(I32, (blocks, W), 1)
+        cosine, sine = cos_sin(mod_phase(outer, column))
+        outside[2 * n] = cosine
+        outside[2 * n + 1] = sine
+
+    def factor(n, k):
+        cosine, sine = outside[2 * n, k : k + 1, :], outside[2 * n + 1, k : k + 1, :]
+        x, y = factors[n]
+        return x * cosine - y * sine, y * cosine + x * sine
+
+    def fill(n):
+        slot = n % 2
+        for k in range(blocks):
+            at = slice(8 * k, 8 * k + 8)
+            twice = None
+            for local in range(chunk // W):
+                stage = (n * (chunk // W) + local) % CHAIN
+                if stage == 0:
+                    if n == 0:
+                        c1, s1 = factor(0, k)
+                    else:
+                        leap_c, leap_s = factor(2, k)
+                        c0, s0 = state[4, at], state[5, at]
+                        c1, s1 = c0 * leap_c - s0 * leap_s, s0 * leap_c + c0 * leap_s
+                    if (n + 1) * chunk < count:
+                        state[4, at], state[5, at] = c1, s1
+                elif stage == 1:
+                    turn_c, turn_s = factor(1, k)
+                    twice = turn_c + turn_c
+                    state[6, at] = twice
+                    c0, s0 = c1, s1
+                    c1, s1 = c0 * turn_c - s0 * turn_s, s0 * turn_c + c0 * turn_s
+                else:
+                    if twice is None:
+                        twice = state[6, at]
+                        c0, s0, c1, s1 = (state[i, at] for i in range(4))
+                    c0, c1 = c1, twice * c1 - c0
+                    s0, s1 = s1, twice * s1 - s0
+                place = slice(local * W, (local + 1) * W)
+                table[slot, at, place] = c1.astype(BF16)
+                table[slot, S + 8 * k : S + 8 * k + 8, place] = s1.astype(BF16)
+            if (n + 1) * (chunk // W) % CHAIN:
+                for i, value in enumerate((c0, s0, c1, s1)):
+                    state[i, at] = value
+
+    fill(0)
     for n in range(steps):
-        for local in range(chunk // W):
-            a = n * (chunk // W) + local
-            c = cos_out[:, a : a + 1]
-            s = sin_out[:, a : a + 1]
-            at = slice(local * W, (local + 1) * W)
-            table[n % 2, 0:S, at] = (c * cos_in - s * sin_in).astype(BF16)
-            table[n % 2, S : 2 * S, at] = (s * cos_in + c * sin_in).astype(BF16)
         copies[n].wait()
+        if n + 1 < steps:
+            fill(n + 1)
         part = slice(n * chunk, (n + 1) * chunk)
         cells = jnp.concatenate([held[0, part, :], held[1, part, :]], axis=1)
         term = jnp.dot(table[n % 2], cells, preferred_element_type=F32)
@@ -121,7 +167,7 @@
 
 def along(strip, row_offsets, facet_offsets, names, facets, cols):
     count = strip.shape[1]
-    chunk = min(1024, count)
+    chunk = min(CHUNK, count)
     rows = S // facets
     slots = names.shape[2]
     return pl.pallas_call(
@@ -134,6 +180,8 @@
             pltpu.VMEM((2, count, W), BF16),
             pltpu.VMEM((2, 2 * S, chunk), BF16),
             pltpu.VMEM((2 * S, 2 * W), F32),
+            pltpu.VMEM((7, S, W), F32),
+            pltpu.VMEM((6, S // 8, W), F32),
             [
                 pltpu.SMEM(facet_offsets.shape, I32),
                 pltpu.SMEM(names.shape, I32),
@@ -249,7 +297,7 @@
     )(columns, got, right)
 
 
-def waves_kernel(facets, uv, right, near, far):
+def waves_kernel(facets, live, uv, right, near, far):
     _, _, inside = split(facets)
     vis = uv.shape[2]
     step = NTOT // UV_STEPS
@@ -265,8 +313,9 @@
         right[j, 2 * TILE : 3 * TILE, :] = (cosine - cos_high.astype(F32)).astype(BF16)
         right[j, 3 * TILE : 4 * TILE, :] = (sine - sin_high.astype(F32)).astype(BF16)
         cosine, sine = cos_sin((uv[j, 0:1, :] * (low * step)) & (NTOT - 1))
-        near[j, 0] = cosine * (1.0 / TILE)
-        near[j, 1] = sine * (1.0 / TILE)
+        size = jnp.where(j < live[0, 0], 1.0 / TILE, 0.0)
+        near[j, 0] = cosine * size
+        near[j, 1] = sine * size
         cosine, sine = cos_sin((uv[j, 0:1, :] * (high * step)) & (NTOT - 1))
         far[j, 0] = cosine
         far[j, 1] = sine
@@ -275,7 +324,7 @@
     lax.fori_loop(0, uv.shape[0], slot, 0)
 
 
-def waves(uv, facets):
+def waves(live, uv, facets):
     slots, _, vis = uv.shape
     return pl.pallas_call(
         functools.partial(waves_kernel, facets),
@@ -284,17 +333,20 @@
             jax.ShapeDtypeStruct((slots, 2, 8, vis), F32),
             jax.ShapeDtypeStruct((slots, 2, 4, vis), F32),
         ),
-        in_specs=[pl.BlockSpec(memory_space=pltpu.VMEM)],
+        in_specs=[
+            pl.BlockSpec(memory_space=pltpu.SMEM),
+            pl.BlockSpec(memory_space=pltpu.VMEM),
+        ],
         out_specs=[pl.BlockSpec(memory_space=pltpu.VMEM)] * 3,
         compiler_params=pltpu.CompilerParams(vmem_limit_bytes=VMEM_LIMIT),
         cost_estimate=pl.CostEstimate(flops=1 << 26, bytes_accessed=3 << 20, transcendentals=0),
         name="waves",
-    )(uv)
-
-
-def visibility_kernel(facets, live, parts, right, near, far, out, held):
+    )(live, uv)
+
+
+def visibility_kernel(facets, parts, right, near, far, out, held):
     groups, _, inside = split(facets)
-    slots, vis = out.shape[0], out.shape[2]
+    slots = out.shape[0]
     sources = facets // groups
     for f in range(sources):
         held[f] = parts[f].astype(F32)
@@ -303,38 +355,31 @@
     lane = lax.broadcasted_iota(I32, (sources, W), 1)
     sign = jnp.where((lane & TILE) == 0, 1.0, -1.0).astype(F32)
     for j in range(slots):
-        @pl.when(j < live[0, 0])
-        def _():
-            x = held[:, j, :]
-            y = pltpu.roll(x, W // 2, 1)
-            both = [jnp.where(lane < W // 2, x, y), jnp.where(lane < W // 2, y, x)][:inside]
-            lhs = [z * sign for z in both] + [pltpu.roll(z, TILE, 1) for z in both]
-            middle = jnp.dot(
-                jnp.concatenate(lhs, axis=0).astype(BF16), right[j], preferred_element_type=F32
-            )
-            real, imag = middle[0:8], middle[TILE : TILE + 8]
-            for h in range(1, 4):
-                more_re = middle[8 * h : 8 * h + 8]
-                more_im = middle[TILE + 8 * h : TILE + 8 * h + 8]
-                cosine, sine = far[j, 0, h : h + 1, :], far[j, 1, h : h + 1, :]
-                real = real + (cosine * more_re - sine * more_im)
-                imag = imag + (cosine * more_im + sine * more_re)
-            cosine, sine = near[j, 0], near[j, 1]
-            out[j, 0:1, :] = jnp.sum(cosine * real - sine * imag, axis=0, keepdims=True)
-            out[j, 1:2, :] = jnp.sum(cosine * imag + sine * real, axis=0, keepdims=True)
-
-        @pl.when(j >= live[0, 0])
-        def _():
-            out[j] = jnp.zeros((2, vis), F32)
-
-
-def visibilities_of(parts, live, tables, facets):
+        x = held[:, j, :]
+        y = pltpu.roll(x, W // 2, 1)
+        both = [jnp.where(lane < W // 2, x, y), jnp.where(lane < W // 2, y, x)][:inside]
+        lhs = [z * sign for z in both] + [pltpu.roll(z, TILE, 1) for z in both]
+        middle = jnp.dot(
+            jnp.concatenate(lhs, axis=0).astype(BF16), right[j], preferred_element_type=F32
+        )
+        real, imag = middle[0:8], middle[TILE : TILE + 8]
+        for h in range(1, 4):
+            more_re = middle[8 * h : 8 * h + 8]
+            more_im = middle[TILE + 8 * h : TILE + 8 * h + 8]
+            cosine, sine = far[j, 0, h : h + 1, :], far[j, 1, h : h + 1, :]
+            real = real + (cosine * more_re - sine * more_im)
+            imag = imag + (cosine * more_im + sine * more_re)
+        cosine, sine = near[j, 0], near[j, 1]
+        out[j, 0:1, :] = jnp.sum(cosine * real - sine * imag, axis=0, keepdims=True)
+        out[j, 1:2, :] = jnp.sum(cosine * imag + sine * real, axis=0, keepdims=True)
+
+
+def visibilities_of(parts, tables, facets):
     slots, _, vis = tables[0].shape
     return pl.pallas_call(
         functools.partial(visibility_kernel, facets),
         out_shape=jax.ShapeDtypeStruct((slots, 2, vis), F32),
-        in_specs=[pl.BlockSpec(memory_space=pltpu.SMEM)]
-        + [pl.BlockSpec(memory_space=pltpu.VMEM)] * 4,
+        in_specs=[pl.BlockSpec(memory_space=pltpu.VMEM)] * 4,
         out_specs=pl.BlockSpec(memory_space=pltpu.VMEM),
         scratch_shapes=[pltpu.VMEM((facets // split(facets)[0], slots, W), F32)],
         compiler_params=pltpu.CompilerParams(vmem_limit_bytes=VMEM_LIMIT),
@@ -342,7 +387,7 @@
             flops=slots * 2 * 64 * 128 * vis, bytes_accessed=1 << 20, transcendentals=0
         ),
         name="visibility",
-    )(live, parts, *tables)
+    )(parts, *tables)
 
 
 def shards(
@@ -352,10 +397,10 @@
     sent = along(facet_strips[0], row_offsets, facet_offsets, tile_lists, facets, cols)
     got = lax.all_to_all(sent, ("facet", "col"), 0, 0, tiled=True)
     right = base(column_offsets)
+    tables = waves(tile_counts, uv_index[0, 0], facets)
     asked = across(got, right, column_offsets, facets, cols)
     parts = lax.all_to_all(asked, "facet", 0, 0, tiled=True)
-    tables = waves(uv_index[0, 0], facets)
-    result = visibilities_of(parts, tile_counts, tables, facets)
+    result = visibilities_of(parts, tables, facets)
     return result[None, None]
 
 

time: 38 us -> 37.4 us (0.984)
  Pallas kernels: 10.8 us -> 10.1 us
    pallas_call x1, Pallas kernels: 5.43 us -> 4.74 us  [along(): pl.pallas_call(functools.partial(along_kernel, facets, cols, chunk), out_...]
where the time goes in v4:
time: 37.4 us; the launch traced here: 37.1 us
  waiting for transfers between devices  14.1 us (38%)
  starting transfers between devices  10.8 us (29%)
  Pallas kernels  10.1 us (27%)
  between operations  2 us (5%)
    all_to_all x1, waiting for transfers between devices, shards(): got = lax.all_to_all(sent, ('facet', 'col'), 0, 0, tiled=True)  10.6 us
    all_to_all x1, starting transfers between devices, shards(): got = lax.all_to_all(sent, ('facet', 'col'), 0, 0, tiled=True)  7.33 us
    pallas_call x1, Pallas kernels, along(): pl.pallas_call(functools.partial(along_kernel, facets, cols, chunk), out_...  4.74 us
    all_to_all x1, waiting for transfers between devices, shards(): parts = lax.all_to_all(asked, 'facet', 0, 0, tiled=True)  3.52 us
    all_to_all x1, starting transfers between devices, shards(): parts = lax.all_to_all(asked, 'facet', 0, 0, tiled=True)  3.5 us
    pallas_call x1, Pallas kernels, waves(): pl.pallas_call(functools.partial(waves_kernel, facets), out_shape=(jax.Sh...  2.42 us
    pallas_call x1, Pallas kernels, visibilities_of(): pl.pallas_call(functools.partial(visibility_kernel, facets), out_shape=ja...  1.46 us
    pallas_call x1, Pallas kernels, across(): pl.pallas_call(functools.partial(across_kernel, facets, cols), out_shape=...  1.12 us
  transfers between devices with their start and end apart: 2, of which 2 were waited for; matrix products, arithmetic and copies ran while one was open for 0% of the time, Pallas kernels for 8%

profile of v4, /device:TPU:0, one launch (start us, length us, event | category | flops | bytes accessed | tf_op | source)
XLA Modules:
  0.0 37.1 jit_solution(7506479959001890499)
XLA Ops:
  0.7 0.0 copy-start
  0.7 4.7 %along.1 = bf16[32,40,128]{2,1,0:T(8,128)(2,1)} custom-call(s32[1]{0:T(128)S(6)} %copy.9.scal, s32[1,2]{1,0:T(1,128)} %offsets.1, s32[1,1,8]{2,1,0:T(1,128)} %names.1, bf16[2,4096,128]{2,1,0:T(8,128)(2,1)} %bitcast.4), custom_call_target="tpu_custom_call" | custom-call | flops 1073741824 | bytes 2097152 | tf_op jit(solution)/shard_map/along/pallas_call | solution.py:173
  5.4 7.3 %all-to-all-start = ((bf16[32,40,128]{2,1,0:T(8,128)(2,1)}), bf16[32,40,128]{2,1,0:T(8,128)(2,1)S(1)}, u32[]{:S(2)}, u32[]{:S(2)}) async-start(bf16[32,40,128]{2,1,0:T(8,128)(2,1)} %along.1), calls=%async_computation | async-start | bytes 655360 | tf_op jit(solution)/shard_map/all_to_all | solution.py:398
  13.4 0.4 %base.1.right = bf16[256,512]{1,0:T(8,128)(2,1)S(1)} custom-call(s32[1]{0:T(128)S(6)} %copy.8.columns), custom_call_target="tpu_custom_call" | custom-call | flops 16777216 | bytes 262144 | tf_op jit(solution)/shard_map/base/pallas_call | solution.py:213
  13.8 10.6 %all-to-all-done.got = bf16[32,40,128]{2,1,0:T(8,128)(2,1)S(1)} async-done(((bf16[32,40,128]{2,1,0:T(8,128)(2,1)}), bf16[32,40,128]{2,1,0:T(8,128)(2,1)S(1)}, u32[]{:S(2)}, u32[]{:S(2)}) %all-to-all-start) | async-done | bytes 327712 | tf_op jit(solution)/shard_map/all_to_all | solution.py:398
  24.4 1.1 %across.1 = bf16[16,8,128]{2,1,0:T(8,128)(2,1)} custom-call(s32[1]{0:T(128)S(6)} %copy.8.columns, bf16[32,40,128]{2,1,0:T(8,128)(2,1)S(1)} %all-to-all-done.got, bf16[256,512]{1,0:T(8,128)(2,1)S(1)} %base.1.right), custom_call_target="tpu_custom_call" | custom-call | flops 134217728 | bytes 1048576 | tf_op jit(solution)/shard_map/across/pallas_call | solution.py:278
  25.6 3.5 %all-to-all-start.1 = ((bf16[16,8,128]{2,1,0:T(8,128)(2,1)}), bf16[16,8,128]{2,1,0:T(8,128)(2,1)S(1)}, u32[]{:S(2)}, u32[]{:S(2)}) async-start(bf16[16,8,128]{2,1,0:T(8,128)(2,1)} %across.1), calls=%async_computation.1 | async-start | bytes 65536 | tf_op jit(solution)/shard_map/all_to_all | solution.py:402
  29.7 0.0 copy-done
  29.7 2.4 %waves.1 = (bf16[8,128,1024]{2,1,0:T(8,128)(2,1)S(1)}, f32[8,2,8,1024]{3,2,1,0:T(8,128)S(1)}, f32[8,2,4,1024]{3,2,1,0:T(4,128)S(1)}) custom-call(s32[1,1]{1,0:T(1,128)S(6)} %copy.10.live, s32[8,2,1024]{2,1,0:T(2,128)S(1)} %bitcast.3), custom_call_target="tpu_custom_call" | custom-call | flops 67108864 | bytes 3145728 | tf_op jit(solution)/shard_map/waves/pallas_call | solution.py:329
  32.2 3.5 %all-to-all-done.1.parts = bf16[16,8,128]{2,1,0:T(8,128)(2,1)S(1)} async-done(((bf16[16,8,128]{2,1,0:T(8,128)(2,1)}), bf16[16,8,128]{2,1,0:T(8,128)(2,1)S(1)}, u32[]{:S(2)}, u32[]{:S(2)}) %all-to-all-start.1) | async-done | bytes 32800 | tf_op jit(solution)/shard_map/all_to_all | solution.py:402
  35.7 1.5 %visibility.1 = f32[8,2,1024]{2,1,0:T(2,128)} custom-call(bf16[16,8,128]{2,1,0:T(8,128)(2,1)S(1)} %all-to-all-done.1.parts, bf16[8,128,1024]{2,1,0:T(8,128)(2,1)S(1)} %get-tuple-element.8.right, f32[8,2,8,1024]{3,2,1,0:T(8,128)S(1)} %get-tuple-element.9.near, f32[8,2,4,1024]{3,2,1,0:T(4,128)S(1)} %get-tuple-element.10.far), custom_call_target="tpu_custom_call" | custom-call | flops 134217728 | bytes 1048576 | tf_op jit(solution)/shard_map/visibility/pallas_call | solution.py:379
Async XLA Ops:
  0.7 29.1 %copy-start = (s32[1,1,8,2,1024]{4,3,2,1,0:T(2,128)S(1)}, s32[1,1,8,2,1024]{4,3,2,1,0:T(2,128)}, u32[]{:S(2)}) copy-start(s32[1,1,8,2,1024]{4,3,2,1,0:T(2,128)} %param.13) | copy-start | bytes 196612
  5.4 19.0 %all-to-all-start = ((bf16[32,40,128]{2,1,0:T(8,128)(2,1)}), bf16[32,40,128]{2,1,0:T(8,128)(2,1)S(1)}, u32[]{:S(2)}, u32[]{:S(2)}) async-start(bf16[32,40,128]{2,1,0:T(8,128)(2,1)} %along.1), calls=%async_computation | async-start | bytes 655360 | tf_op jit(solution)/shard_map/all_to_all | solution.py:398
  25.6 10.1 %all-to-all-start.1 = ((bf16[16,8,128]{2,1,0:T(8,128)(2,1)}), bf16[16,8,128]{2,1,0:T(8,128)(2,1)S(1)}, u32[]{:S(2)}, u32[]{:S(2)}) async-start(bf16[16,8,128]{2,1,0:T(8,128)(2,1)} %across.1), calls=%async_computation.1 | async-start | bytes 65536 | tf_op jit(solution)/shard_map/all_to_all | solution.py:402

commit v5 on v4

--- a/solution.py
+++ b/solution.py
@@ -18,6 +18,7 @@
 VMEM_LIMIT = 16 << 20
 CHUNK = 512
 CHAIN = 16
+AHEAD = 4
 BF16 = jnp.bfloat16
 F32 = jnp.float32
 I32 = jnp.int32
@@ -63,10 +64,7 @@
         part = pl.ds(n * chunk, chunk)
         copies.append(pltpu.make_async_copy(strip.at[:, part], held.at[:, part], sems.at[n]))
         copies[n].start()
-    for copy in notes:
-        copy.wait()
     row_start = scal[0]
-    col_start = small[0][0, 0] + lax.axis_index("col") * count
     rows = S // facets
     groups, tall, inside = split(facets)
 
@@ -80,15 +78,12 @@
     blocks = S // 8
     inner = row_start + (NTOT // L) * sample_of(lax.broadcasted_iota(I32, (8, W), 0))
     outer = (NTOT // L) * sample_of(8 * lax.broadcasted_iota(I32, (blocks, W), 0))
-    cell = col_start + lax.broadcasted_iota(I32, (8, W), 1)
-    cells_of = {"first": (cell, 1.0 / math.sqrt(L)), "step": (W, 1.0), "leap": (CHAIN * W, 1.0)}
-    factors = []
-    for n, (column, scale) in enumerate(cells_of.values()):
+    factors = {}
+
+    def factor_tables(n, column, wide_column, scale):
         cosine, sine = cos_sin(mod_phase(inner, column))
-        factors.append((cosine * scale, sine * scale))
-        if n == 0:
-            column = col_start + lax.broadcasted_iota(I32, (blocks, W), 1)
-        cosine, sine = cos_sin(mod_phase(outer, column))
+        factors[n] = (cosine * scale, sine * scale)
+        cosine, sine = cos_sin(mod_phase(outer, wide_column))
         outside[2 * n] = cosine
         outside[2 * n + 1] = sine
 
@@ -97,8 +92,19 @@
         x, y = factors[n]
         return x * cosine - y * sine, y * cosine + x * sine
 
+    factor_tables(1, W, W, 1.0)
+    factor_tables(2, CHAIN * W, CHAIN * W, 1.0)
+    notes[0].wait()
+    col_start = small[0][0, 0] + lax.axis_index("col") * count
+    factor_tables(
+        0,
+        col_start + lax.broadcasted_iota(I32, (8, W), 1),
+        col_start + lax.broadcasted_iota(I32, (blocks, W), 1),
+        1.0 / math.sqrt(L),
+    )
+
     def fill(n):
-        slot = n % 2
+        slot = n % (AHEAD + 1)
         for k in range(blocks):
             at = slice(8 * k, 8 * k + 8)
             twice = None
@@ -132,14 +138,17 @@
                 for i, value in enumerate((c0, s0, c1, s1)):
                     state[i, at] = value
 
-    fill(0)
+    ahead = min(AHEAD, steps)
+    for n in range(ahead):
+        fill(n)
+    for copy in copies:
+        copy.wait()
     for n in range(steps):
-        copies[n].wait()
-        if n + 1 < steps:
-            fill(n + 1)
+        if n + ahead < steps:
+            fill(n + ahead)
         part = slice(n * chunk, (n + 1) * chunk)
         cells = jnp.concatenate([held[0, part, :], held[1, part, :]], axis=1)
-        term = jnp.dot(table[n % 2], cells, preferred_element_type=F32)
+        term = jnp.dot(table[n % (AHEAD + 1)], cells, preferred_element_type=F32)
         if n == 0:
             total[...] = term
         else:
@@ -148,6 +157,7 @@
     imag = total[0:S, W : 2 * W] - total[S : 2 * S, 0:W]
     total[0:S, 0:W] = real
     total[0:S, W : 2 * W] = imag
+    notes[1].wait()
     across = small[0][0, 1]
     line = lax.broadcasted_iota(I32, (slots, W), 0)
     spot = lax.broadcasted_iota(I32, (slots, W), 1)
@@ -178,7 +188,7 @@
         out_specs=pl.BlockSpec(memory_space=pltpu.VMEM),
         scratch_shapes=[
             pltpu.VMEM((2, count, W), BF16),
-            pltpu.VMEM((2, 2 * S, chunk), BF16),
+            pltpu.VMEM((AHEAD + 1, 2 * S, chunk), BF16),
             pltpu.VMEM((2 * S, 2 * W), F32),
             pltpu.VMEM((7, S, W), F32),
             pltpu.VMEM((6, S // 8, W), F32),

time: 37.4 us -> 36.5 us (0.976)
  Pallas kernels: 10.1 us -> 9.21 us
    pallas_call x1, Pallas kernels: 4.74 us -> 3.8 us  [along(): pl.pallas_call(functools.partial(along_kernel, facets, cols, chunk), out_...]
where the time goes in v5:
time: 36.5 us; the launch traced here: 36.2 us
  waiting for transfers between devices  14.1 us (39%)
  starting transfers between devices  10.8 us (30%)
  Pallas kernels  9.21 us (25%)
  between operations  2 us (5%)
    all_to_all x1, waiting for transfers between devices, shards(): got = lax.all_to_all(sent, ('facet', 'col'), 0, 0, tiled=True)  10.6 us
    all_to_all x1, starting transfers between devices, shards(): got = lax.all_to_all(sent, ('facet', 'col'), 0, 0, tiled=True)  7.33 us
    pallas_call x1, Pallas kernels, along(): pl.pallas_call(functools.partial(along_kernel, facets, cols, chunk), out_...  3.8 us
    all_to_all x1, waiting for transfers between devices, shards(): parts = lax.all_to_all(asked, 'facet', 0, 0, tiled=True)  3.52 us
    all_to_all x1, starting transfers between devices, shards(): parts = lax.all_to_all(asked, 'facet', 0, 0, tiled=True)  3.5 us
    pallas_call x1, Pallas kernels, waves(): pl.pallas_call(functools.partial(waves_kernel, facets), out_shape=(jax.Sh...  2.42 us
    pallas_call x1, Pallas kernels, visibilities_of(): pl.pallas_call(functools.partial(visibility_kernel, facets), out_shape=ja...  1.46 us
    pallas_call x1, Pallas kernels, across(): pl.pallas_call(functools.partial(across_kernel, facets, cols), out_shape=...  1.12 us
  transfers between devices with their start and end apart: 2, of which 2 were waited for; matrix products, arithmetic and copies ran while one was open for 0% of the time, Pallas kernels for 8%

profile of v5, /device:TPU:0, one launch (start us, length us, event | category | flops | bytes accessed | tf_op | source)
XLA Modules:
  0.0 36.2 jit_solution(4047745401787477305)
XLA Ops:
  0.7 0.0 copy-start
  0.7 3.8 %along.1 = bf16[32,40,128]{2,1,0:T(8,128)(2,1)} custom-call(s32[1]{0:T(128)S(6)} %copy.9.scal, s32[1,2]{1,0:T(1,128)} %offsets.1, s32[1,1,8]{2,1,0:T(1,128)} %names.1, bf16[2,4096,128]{2,1,0:T(8,128)(2,1)} %bitcast.4), custom_call_target="tpu_custom_call" | custom-call | flops 1073741824 | bytes 2097152 | tf_op jit(solution)/shard_map/along/pallas_call | solution.py:183
  4.5 7.3 %all-to-all-start = ((bf16[32,40,128]{2,1,0:T(8,128)(2,1)}), bf16[32,40,128]{2,1,0:T(8,128)(2,1)S(1)}, u32[]{:S(2)}, u32[]{:S(2)}) async-start(bf16[32,40,128]{2,1,0:T(8,128)(2,1)} %along.1), calls=%async_computation | async-start | bytes 655360 | tf_op jit(solution)/shard_map/all_to_all | solution.py:408
  12.5 0.4 %base.1.right = bf16[256,512]{1,0:T(8,128)(2,1)S(1)} custom-call(s32[1]{0:T(128)S(6)} %copy.8.columns), custom_call_target="tpu_custom_call" | custom-call | flops 16777216 | bytes 262144 | tf_op jit(solution)/shard_map/base/pallas_call | solution.py:223
  12.9 10.6 %all-to-all-done.got = bf16[32,40,128]{2,1,0:T(8,128)(2,1)S(1)} async-done(((bf16[32,40,128]{2,1,0:T(8,128)(2,1)}), bf16[32,40,128]{2,1,0:T(8,128)(2,1)S(1)}, u32[]{:S(2)}, u32[]{:S(2)}) %all-to-all-start) | async-done | bytes 327712 | tf_op jit(solution)/shard_map/all_to_all | solution.py:408
  23.5 1.1 %across.1 = bf16[16,8,128]{2,1,0:T(8,128)(2,1)} custom-call(s32[1]{0:T(128)S(6)} %copy.8.columns, bf16[32,40,128]{2,1,0:T(8,128)(2,1)S(1)} %all-to-all-done.got, bf16[256,512]{1,0:T(8,128)(2,1)S(1)} %base.1.right), custom_call_target="tpu_custom_call" | custom-call | flops 134217728 | bytes 1048576 | tf_op jit(solution)/shard_map/across/pallas_call | solution.py:288
  24.6 3.5 %all-to-all-start.1 = ((bf16[16,8,128]{2,1,0:T(8,128)(2,1)}), bf16[16,8,128]{2,1,0:T(8,128)(2,1)S(1)}, u32[]{:S(2)}, u32[]{:S(2)}) async-start(bf16[16,8,128]{2,1,0:T(8,128)(2,1)} %across.1), calls=%async_computation.1 | async-start | bytes 65536 | tf_op jit(solution)/shard_map/all_to_all | solution.py:412
  28.8 0.0 copy-done
  28.8 2.4 %waves.1 = (bf16[8,128,1024]{2,1,0:T(8,128)(2,1)S(1)}, f32[8,2,8,1024]{3,2,1,0:T(8,128)S(1)}, f32[8,2,4,1024]{3,2,1,0:T(4,128)S(1)}) custom-call(s32[1,1]{1,0:T(1,128)S(6)} %copy.10.live, s32[8,2,1024]{2,1,0:T(2,128)S(1)} %bitcast.3), custom_call_target="tpu_custom_call" | custom-call | flops 67108864 | bytes 3145728 | tf_op jit(solution)/shard_map/waves/pallas_call | solution.py:339
  31.2 3.5 %all-to-all-done.1.parts = bf16[16,8,128]{2,1,0:T(8,128)(2,1)S(1)} async-done(((bf16[16,8,128]{2,1,0:T(8,128)(2,1)}), bf16[16,8,128]{2,1,0:T(8,128)(2,1)S(1)}, u32[]{:S(2)}, u32[]{:S(2)}) %all-to-all-start.1) | async-done | bytes 32800 | tf_op jit(solution)/shard_map/all_to_all | solution.py:412
  34.7 1.5 %visibility.1 = f32[8,2,1024]{2,1,0:T(2,128)} custom-call(bf16[16,8,128]{2,1,0:T(8,128)(2,1)S(1)} %all-to-all-done.1.parts, bf16[8,128,1024]{2,1,0:T(8,128)(2,1)S(1)} %get-tuple-element.8.right, f32[8,2,8,1024]{3,2,1,0:T(8,128)S(1)} %get-tuple-element.9.near, f32[8,2,4,1024]{3,2,1,0:T(4,128)S(1)} %get-tuple-element.10.far), custom_call_target="tpu_custom_call" | custom-call | flops 134217728 | bytes 1048576 | tf_op jit(solution)/shard_map/visibility/pallas_call | solution.py:389
Async XLA Ops:
  0.7 28.1 %copy-start = (s32[1,1,8,2,1024]{4,3,2,1,0:T(2,128)S(1)}, s32[1,1,8,2,1024]{4,3,2,1,0:T(2,128)}, u32[]{:S(2)}) copy-start(s32[1,1,8,2,1024]{4,3,2,1,0:T(2,128)} %param.13) | copy-start | bytes 196612
  4.5 19.0 %all-to-all-start = ((bf16[32,40,128]{2,1,0:T(8,128)(2,1)}), bf16[32,40,128]{2,1,0:T(8,128)(2,1)S(1)}, u32[]{:S(2)}, u32[]{:S(2)}) async-start(bf16[32,40,128]{2,1,0:T(8,128)(2,1)} %along.1), calls=%async_computation | async-start | bytes 655360 | tf_op jit(solution)/shard_map/all_to_all | solution.py:408
  24.6 10.1 %all-to-all-start.1 = ((bf16[16,8,128]{2,1,0:T(8,128)(2,1)}), bf16[16,8,128]{2,1,0:T(8,128)(2,1)S(1)}, u32[]{:S(2)}, u32[]{:S(2)}) async-start(bf16[16,8,128]{2,1,0:T(8,128)(2,1)} %across.1), calls=%async_computation.1 | async-start | bytes 65536 | tf_op jit(solution)/shard_map/all_to_all | solution.py:412

commit v6 on v5

--- a/solution.py
+++ b/solution.py
@@ -159,30 +159,28 @@
     total[0:S, W : 2 * W] = imag
     notes[1].wait()
     across = small[0][0, 1]
-    line = lax.broadcasted_iota(I32, (slots, W), 0)
-    spot = lax.broadcasted_iota(I32, (slots, W), 1)
-    note = jnp.zeros((slots, W), I32)
+    spot = lax.broadcasted_iota(I32, (2, W), 1)
+    note = jnp.where(spot == W - 2, across >> 8, jnp.where(spot == W - 1, across & 255, 0))
     for j in range(slots):
-        note = jnp.where(line == j, small[1][0, 0, j], note)
-    note = jnp.where(spot == W - 2, across >> 8, jnp.where(spot == W - 1, across & 255, note))
+        note = jnp.where(spot == j, small[1][0, 0, j], note)
     note = note.astype(F32).astype(BF16)
     for o in range(facets):
         re = total[o * rows : (o + 1) * rows, 0:W].astype(BF16)
         im = total[o * rows : (o + 1) * rows, W : 2 * W].astype(BF16)
         for c in range(cols):
-            out[o * cols + c, 0:rows, :] = re
-            out[o * cols + c, rows : 2 * rows, :] = im
-            out[o * cols + c, 2 * rows :, :] = note
+            at = (o * cols + c) * (2 * rows + 2)
+            out[at : at + rows, :] = re
+            out[at + rows : at + 2 * rows, :] = im
+            out[at + 2 * rows : at + 2 * rows + 2, :] = note
 
 
 def along(strip, row_offsets, facet_offsets, names, facets, cols):
     count = strip.shape[1]
     chunk = min(CHUNK, count)
     rows = S // facets
-    slots = names.shape[2]
     return pl.pallas_call(
         functools.partial(along_kernel, facets, cols, chunk),
-        out_shape=jax.ShapeDtypeStruct((facets * cols, 2 * rows + slots, W), BF16),
+        out_shape=jax.ShapeDtypeStruct((facets * cols * (2 * rows + 2), W), BF16),
         in_specs=[pl.BlockSpec(memory_space=pltpu.SMEM)]
         + [pl.BlockSpec(memory_space=pltpu.HBM)] * 3,
         out_specs=pl.BlockSpec(memory_space=pltpu.VMEM),
@@ -234,24 +232,33 @@
 def across_kernel(facets, cols, columns, got, right, out, left, summed, phases):
     rows = S // facets
     groups, tall, inside = split(facets)
-    slots = got.shape[1] - 2 * rows
+    slots = out.shape[1]
     wide = 2 * S
     height = facets * rows
+    size = 2 * rows + 2
     column = lax.axis_index("col")
     sources = []
     for f in range(facets):
-        re = got[f * cols, 0:rows, :].astype(F32)
-        im = got[f * cols, rows : 2 * rows, :].astype(F32)
-        for h in range(1, cols):
-            re = re + got[f * cols + h, 0:rows, :].astype(F32)
-            im = im + got[f * cols + h, rows : 2 * rows, :].astype(F32)
+        parts = []
+        for part in range(2):
+            at = f * cols * size + part * rows
+            value = got[at : at + rows, :].astype(F32)
+            for h in range(1, cols):
+                value = value + got[at + h * size : at + h * size + rows, :].astype(F32)
+            parts.append(value)
+        re, im = parts
         left[f * rows : (f + 1) * rows, 0:W] = re
         left[f * rows : (f + 1) * rows, W : 2 * W] = im
         left[height + f * rows : height + (f + 1) * rows, 0:W] = im
         left[height + f * rows : height + (f + 1) * rows, W : 2 * W] = -re
-        sources.append(got[f * cols + column, 2 * rows :, :].astype(F32))
+        note = None
+        for h in range(cols):
+            at = (f * cols + h) * size + 2 * rows
+            value = jnp.where(column == h, got[at : at + 2, :].astype(F32)[0:1], 0.0)
+            note = value if note is None else note + value
+        sources.append(note)
     summed[...] = jnp.dot(left[...].astype(BF16), right[...], preferred_element_type=F32)
-    heads = jnp.concatenate([note[0:1] for note in sources], axis=0)
+    heads = jnp.concatenate(sources, axis=0)
     offset = (heads[:, W - 2 : W - 1] * 256.0 + heads[:, W - 1 : W]).astype(I32)
     lane = lax.broadcasted_iota(I32, (facets, wide), 1)
     cosine, sine = cos_sin(mod_phase(offset, positions(columns[0], lane)))
@@ -270,7 +277,13 @@
             parts.append(jnp.zeros_like(parts[0]))
         pieces.append(jnp.concatenate(parts, axis=1))
     tiles = jnp.concatenate(pieces, axis=0).astype(BF16)
-    names = jnp.concatenate(sources, axis=0).astype(I32)
+    line = lax.broadcasted_iota(I32, (facets * slots, facets), 0)
+    place = line - slots * lax.broadcasted_iota(I32, line.shape, 1)
+    owner = jnp.where((place >= 0) & (place < slots), 1.0, 0.0)
+    spread = jnp.dot(owner.astype(BF16), heads.astype(BF16), preferred_element_type=F32)
+    line = lax.broadcasted_iota(I32, spread.shape, 0)
+    own = lax.broadcasted_iota(I32, spread.shape, 1) == (line & (slots - 1))
+    names = jnp.sum(jnp.where(own, spread, 0.0), axis=1, keepdims=True).astype(I32)
     first = (lax.axis_index("facet") // (facets // groups)) * tall
     local = (names >> 3) - first
     wanted = jnp.where((local >= 0) & (local < tall), (names & 7) * tall + local, -1)
@@ -282,9 +295,7 @@
         out[o] = chosen[o * slots : (o + 1) * slots, :].astype(BF16)
 
 
-def across(got, right, columns, facets, cols):
-    rows = S // facets
-    slots = got.shape[1] - 2 * rows
+def across(got, right, columns, slots, facets, cols):
     return pl.pallas_call(
         functools.partial(across_kernel, facets, cols),
         out_shape=jax.ShapeDtypeStruct((facets, slots, W), BF16),
@@ -405,10 +416,12 @@
 ):
     facets, cols = lax.axis_size("facet"), lax.axis_size("col")
     sent = along(facet_strips[0], row_offsets, facet_offsets, tile_lists, facets, cols)
-    got = lax.all_to_all(sent, ("facet", "col"), 0, 0, tiled=True)
+    pairs = sent.reshape((facets * cols, -1, 2, W))
+    got = lax.all_to_all(pairs, ("facet", "col"), 0, 0, tiled=True)
+    got = got.reshape(sent.shape)
     right = base(column_offsets)
     tables = waves(tile_counts, uv_index[0, 0], facets)
-    asked = across(got, right, column_offsets, facets, cols)
+    asked = across(got, right, column_offsets, tile_lists.shape[2], facets, cols)
     parts = lax.all_to_all(asked, "facet", 0, 0, tiled=True)
     result = visibilities_of(parts, tables, facets)
     return result[None, None]

time: 36.5 us -> 35.8 us (0.981)
  waiting for transfers between devices: 14.1 us -> 13.4 us
    all_to_all x1, waiting for transfers between devices: 10.6 us -> 9.86 us  [shards(): got = lax.all_to_all(pairs, ('facet', 'col'), 0, 0, tiled=True)]
where the time goes in v6:
time: 35.8 us; the launch traced here: 35.5 us
  waiting for transfers between devices  13.4 us (37%)
  starting transfers between devices  10.8 us (30%)
  Pallas kernels  9.34 us (26%)
  between operations  2 us (6%)
    all_to_all x1, waiting for transfers between devices, shards(): got = lax.all_to_all(pairs, ('facet', 'col'), 0, 0, tiled=True)  9.86 us
    all_to_all x1, starting transfers between devices, shards(): got = lax.all_to_all(pairs, ('facet', 'col'), 0, 0, tiled=True)  7.33 us
    pallas_call x1, Pallas kernels, along(): pl.pallas_call(functools.partial(along_kernel, facets, cols, chunk), out_...  3.82 us
    all_to_all x1, waiting for transfers between devices, shards(): parts = lax.all_to_all(asked, 'facet', 0, 0, tiled=True)  3.52 us
    all_to_all x1, starting transfers between devices, shards(): parts = lax.all_to_all(asked, 'facet', 0, 0, tiled=True)  3.5 us
    pallas_call x1, Pallas kernels, waves(): pl.pallas_call(functools.partial(waves_kernel, facets), out_shape=(jax.Sh...  2.42 us
    pallas_call x1, Pallas kernels, visibilities_of(): pl.pallas_call(functools.partial(visibility_kernel, facets), out_shape=ja...  1.46 us
    pallas_call x1, Pallas kernels, across(): pl.pallas_call(functools.partial(across_kernel, facets, cols), out_shape=...  1.23 us
  transfers between devices with their start and end apart: 2, of which 2 were waited for; matrix products, arithmetic and copies ran while one was open for 0% of the time, Pallas kernels for 8%

profile of v6, /device:TPU:0, one launch (start us, length us, event | category | flops | bytes accessed | tf_op | source)
XLA Modules:
  0.0 35.5 jit_solution(11002024074996394731)
XLA Ops:
  0.7 0.0 copy-start
  0.7 3.8 %along.1 = bf16[1088,128]{1,0:T(8,128)(2,1)} custom-call(s32[1]{0:T(128)S(6)} %copy.9.scal, s32[1,2]{1,0:T(1,128)} %offsets.1, s32[1,1,8]{2,1,0:T(1,128)} %names.1, bf16[2,4096,128]{2,1,0:T(8,128)(2,1)} %bitcast.8), custom_call_target="tpu_custom_call" | custom-call | flops 1073741824 | bytes 2097152 | tf_op jit(solution)/shard_map/along/pallas_call | solution.py:181
  4.5 7.3 %all-to-all-start = ((bf16[32,17,2,128]{3,2,1,0:T(2,128)(2,1)}), bf16[32,17,2,128]{3,2,1,0:T(2,128)(2,1)S(1)}, u32[]{:S(2)}, u32[]{:S(2)}) async-start(bf16[32,17,2,128]{3,2,1,0:T(2,128)(2,1)} %bitcast.7), calls=%async_computation | async-start | bytes 557056 | tf_op jit(solution)/shard_map/all_to_all | solution.py:420
  12.5 0.4 %base.1.right = bf16[256,512]{1,0:T(8,128)(2,1)S(1)} custom-call(s32[1]{0:T(128)S(6)} %copy.8.columns), custom_call_target="tpu_custom_call" | custom-call | flops 16777216 | bytes 262144 | tf_op jit(solution)/shard_map/base/pallas_call | solution.py:221
  12.9 9.9 %all-to-all-done = bf16[32,17,2,128]{3,2,1,0:T(2,128)(2,1)S(1)} async-done(((bf16[32,17,2,128]{3,2,1,0:T(2,128)(2,1)}), bf16[32,17,2,128]{3,2,1,0:T(2,128)(2,1)S(1)}, u32[]{:S(2)}, u32[]{:S(2)}) %all-to-all-start) | async-done | bytes 278560 | tf_op jit(solution)/shard_map/all_to_all | solution.py:420
  22.8 1.2 %across.1 = bf16[16,8,128]{2,1,0:T(8,128)(2,1)} custom-call(s32[1]{0:T(128)S(6)} %copy.8.columns, bf16[1088,128]{1,0:T(8,128)(2,1)S(1)} %bitcast.5, bf16[256,512]{1,0:T(8,128)(2,1)S(1)} %base.1.right), custom_call_target="tpu_custom_call" | custom-call | flops 134217728 | bytes 1048576 | tf_op jit(solution)/shard_map/across/pallas_call | solution.py:299
  24.0 3.5 %all-to-all-start.1 = ((bf16[16,8,128]{2,1,0:T(8,128)(2,1)}), bf16[16,8,128]{2,1,0:T(8,128)(2,1)S(1)}, u32[]{:S(2)}, u32[]{:S(2)}) async-start(bf16[16,8,128]{2,1,0:T(8,128)(2,1)} %across.1), calls=%async_computation.1 | async-start | bytes 65536 | tf_op jit(solution)/shard_map/all_to_all | solution.py:425
  28.1 0.0 copy-done
  28.1 2.4 %waves.1 = (bf16[8,128,1024]{2,1,0:T(8,128)(2,1)S(1)}, f32[8,2,8,1024]{3,2,1,0:T(8,128)S(1)}, f32[8,2,4,1024]{3,2,1,0:T(4,128)S(1)}) custom-call(s32[1,1]{1,0:T(1,128)S(6)} %copy.10.live, s32[8,2,1024]{2,1,0:T(2,128)S(1)} %bitcast.6), custom_call_target="tpu_custom_call" | custom-call | flops 67108864 | bytes 3145728 | tf_op jit(solution)/shard_map/waves/pallas_call | solution.py:350
  30.6 3.5 %all-to-all-done.1.parts = bf16[16,8,128]{2,1,0:T(8,128)(2,1)S(1)} async-done(((bf16[16,8,128]{2,1,0:T(8,128)(2,1)}), bf16[16,8,128]{2,1,0:T(8,128)(2,1)S(1)}, u32[]{:S(2)}, u32[]{:S(2)}) %all-to-all-start.1) | async-done | bytes 32800 | tf_op jit(solution)/shard_map/all_to_all | solution.py:425
  34.1 1.5 %visibility.1 = f32[8,2,1024]{2,1,0:T(2,128)} custom-call(bf16[16,8,128]{2,1,0:T(8,128)(2,1)S(1)} %all-to-all-done.1.parts, bf16[8,128,1024]{2,1,0:T(8,128)(2,1)S(1)} %get-tuple-element.8.right, f32[8,2,8,1024]{3,2,1,0:T(8,128)S(1)} %get-tuple-element.9.near, f32[8,2,4,1024]{3,2,1,0:T(4,128)S(1)} %get-tuple-element.10.far), custom_call_target="tpu_custom_call" | custom-call | flops 134217728 | bytes 1048576 | tf_op jit(solution)/shard_map/visibility/pallas_call | solution.py:400
Async XLA Ops:
  0.7 27.5 %copy-start = (s32[1,1,8,2,1024]{4,3,2,1,0:T(2,128)S(1)}, s32[1,1,8,2,1024]{4,3,2,1,0:T(2,128)}, u32[]{:S(2)}) copy-start(s32[1,1,8,2,1024]{4,3,2,1,0:T(2,128)} %param.13) | copy-start | bytes 196612
  4.5 18.3 %all-to-all-start = ((bf16[32,17,2,128]{3,2,1,0:T(2,128)(2,1)}), bf16[32,17,2,128]{3,2,1,0:T(2,128)(2,1)S(1)}, u32[]{:S(2)}, u32[]{:S(2)}) async-start(bf16[32,17,2,128]{3,2,1,0:T(2,128)(2,1)} %bitcast.7), calls=%async_computation | async-start | bytes 557056 | tf_op jit(solution)/shard_map/all_to_all | solution.py:420
  24.0 10.1 %all-to-all-start.1 = ((bf16[16,8,128]{2,1,0:T(8,128)(2,1)}), bf16[16,8,128]{2,1,0:T(8,128)(2,1)S(1)}, u32[]{:S(2)}, u32[]{:S(2)}) async-start(bf16[16,8,128]{2,1,0:T(8,128)(2,1)} %across.1), calls=%async_computation.1 | async-start | bytes 65536 | tf_op jit(solution)/shard_map/all_to_all | solution.py:425

commit v7 on v6

--- a/solution.py
+++ b/solution.py
@@ -16,9 +16,9 @@
 NTOT = 65536
 UV_STEPS = 4096
 VMEM_LIMIT = 16 << 20
-CHUNK = 512
-CHAIN = 16
-AHEAD = 4
+CHUNK = 4096
+CHAIN = 32
+AHEAD = 1
 BF16 = jnp.bfloat16
 F32 = jnp.float32
 I32 = jnp.int32
@@ -148,11 +148,12 @@
             fill(n + ahead)
         part = slice(n * chunk, (n + 1) * chunk)
         cells = jnp.concatenate([held[0, part, :], held[1, part, :]], axis=1)
-        term = jnp.dot(table[n % (AHEAD + 1)], cells, preferred_element_type=F32)
-        if n == 0:
-            total[...] = term
-        else:
-            total[...] += term
+        for at in (slice(0, S), slice(S, 2 * S)):
+            term = jnp.dot(table[n % (AHEAD + 1), at, :], cells, preferred_element_type=F32)
+            if n == 0:
+                total[at, :] = term
+            else:
+                total[at, :] += term
     real = total[0:S, 0:W] + total[S : 2 * S, W : 2 * W]
     imag = total[0:S, W : 2 * W] - total[S : 2 * S, 0:W]
     total[0:S, 0:W] = real
@@ -168,7 +169,7 @@
         re = total[o * rows : (o + 1) * rows, 0:W].astype(BF16)
         im = total[o * rows : (o + 1) * rows, W : 2 * W].astype(BF16)
         for c in range(cols):
-            at = (o * cols + c) * (2 * rows + 2)
+            at = (c * facets + o) * (2 * rows + 2)
             out[at : at + rows, :] = re
             out[at + rows : at + 2 * rows, :] = im
             out[at + 2 * rows : at + 2 * rows + 2, :] = note
@@ -241,10 +242,11 @@
     for f in range(facets):
         parts = []
         for part in range(2):
-            at = f * cols * size + part * rows
+            at = f * size + part * rows
             value = got[at : at + rows, :].astype(F32)
             for h in range(1, cols):
-                value = value + got[at + h * size : at + h * size + rows, :].astype(F32)
+                step = at + h * facets * size
+                value = value + got[step : step + rows, :].astype(F32)
             parts.append(value)
         re, im = parts
         left[f * rows : (f + 1) * rows, 0:W] = re
@@ -253,7 +255,7 @@
         left[height + f * rows : height + (f + 1) * rows, W : 2 * W] = -re
         note = None
         for h in range(cols):
-            at = (f * cols + h) * size + 2 * rows
+            at = (h * facets + f) * size + 2 * rows
             value = jnp.where(column == h, got[at : at + 2, :].astype(F32)[0:1], 0.0)
             note = value if note is None else note + value
         sources.append(note)
@@ -417,7 +419,7 @@
     facets, cols = lax.axis_size("facet"), lax.axis_size("col")
     sent = along(facet_strips[0], row_offsets, facet_offsets, tile_lists, facets, cols)
     pairs = sent.reshape((facets * cols, -1, 2, W))
-    got = lax.all_to_all(pairs, ("facet", "col"), 0, 0, tiled=True)
+    got = lax.all_to_all(pairs, ("col", "facet"), 0, 0, tiled=True)
     got = got.reshape(sent.shape)
     right = base(column_offsets)
     tables = waves(tile_counts, uv_index[0, 0], facets)

time: 35.8 us -> 35.6 us (level)
  no operation moved by 1% of the time
where the time goes in v7:
time: 35.6 us; the launch traced here: 35.3 us
  waiting for transfers between devices  13.1 us (37%)
  starting transfers between devices  10.8 us (30%)
  Pallas kernels  9.36 us (26%)
  between operations  2 us (6%)
    all_to_all x1, waiting for transfers between devices, shards(): got = lax.all_to_all(pairs, ('col', 'facet'), 0, 0, tiled=True)  9.59 us
    all_to_all x1, starting transfers between devices, shards(): got = lax.all_to_all(pairs, ('col', 'facet'), 0, 0, tiled=True)  7.33 us
    pallas_call x1, Pallas kernels, along(): pl.pallas_call(functools.partial(along_kernel, facets, cols, chunk), out_...  3.84 us
    all_to_all x1, waiting for transfers between devices, shards(): parts = lax.all_to_all(asked, 'facet', 0, 0, tiled=True)  3.54 us
    all_to_all x1, starting transfers between devices, shards(): parts = lax.all_to_all(asked, 'facet', 0, 0, tiled=True)  3.5 us
    pallas_call x1, Pallas kernels, waves(): pl.pallas_call(functools.partial(waves_kernel, facets), out_shape=(jax.Sh...  2.42 us
    pallas_call x1, Pallas kernels, visibilities_of(): pl.pallas_call(functools.partial(visibility_kernel, facets), out_shape=ja...  1.46 us
    pallas_call x1, Pallas kernels, across(): pl.pallas_call(functools.partial(across_kernel, facets, cols), out_shape=...  1.23 us
  transfers between devices with their start and end apart: 2, of which 2 were waited for; matrix products, arithmetic and copies ran while one was open for 0% of the time, Pallas kernels for 8%

profile of v7, /device:TPU:0, one launch (start us, length us, event | category | flops | bytes accessed | tf_op | source)
XLA Modules:
  0.0 35.3 jit_solution(13886766606539235447)
XLA Ops:
  0.7 0.0 copy-start
  0.7 3.8 %along.1 = bf16[1088,128]{1,0:T(8,128)(2,1)} custom-call(s32[1]{0:T(128)S(6)} %copy.9.scal, s32[1,2]{1,0:T(1,128)} %offsets.1, s32[1,1,8]{2,1,0:T(1,128)} %names.1, bf16[2,4096,128]{2,1,0:T(8,128)(2,1)} %bitcast.8), custom_call_target="tpu_custom_call" | custom-call | flops 1073741824 | bytes 2097152 | tf_op jit(solution)/shard_map/along/pallas_call | solution.py:182
  4.5 7.3 %all-to-all-start = ((bf16[32,17,2,128]{3,2,1,0:T(2,128)(2,1)}), bf16[32,17,2,128]{3,2,1,0:T(2,128)(2,1)S(1)}, u32[]{:S(2)}, u32[]{:S(2)}) async-start(bf16[32,17,2,128]{3,2,1,0:T(2,128)(2,1)} %bitcast.7), calls=%async_computation | async-start | bytes 557056 | tf_op jit(solution)/shard_map/all_to_all | solution.py:422
  12.5 0.4 %base.1.right = bf16[256,512]{1,0:T(8,128)(2,1)S(1)} custom-call(s32[1]{0:T(128)S(6)} %copy.8.columns), custom_call_target="tpu_custom_call" | custom-call | flops 16777216 | bytes 262144 | tf_op jit(solution)/shard_map/base/pallas_call | solution.py:222
  12.9 9.6 %all-to-all-done = bf16[32,17,2,128]{3,2,1,0:T(2,128)(2,1)S(1)} async-done(((bf16[32,17,2,128]{3,2,1,0:T(2,128)(2,1)}), bf16[32,17,2,128]{3,2,1,0:T(2,128)(2,1)S(1)}, u32[]{:S(2)}, u32[]{:S(2)}) %all-to-all-start) | async-done | bytes 278560 | tf_op jit(solution)/shard_map/all_to_all | solution.py:422
  22.5 1.2 %across.1 = bf16[16,8,128]{2,1,0:T(8,128)(2,1)} custom-call(s32[1]{0:T(128)S(6)} %copy.8.columns, bf16[1088,128]{1,0:T(8,128)(2,1)S(1)} %bitcast.5, bf16[256,512]{1,0:T(8,128)(2,1)S(1)} %base.1.right), custom_call_target="tpu_custom_call" | custom-call | flops 134217728 | bytes 1048576 | tf_op jit(solution)/shard_map/across/pallas_call | solution.py:301
  23.7 3.5 %all-to-all-start.1 = ((bf16[16,8,128]{2,1,0:T(8,128)(2,1)}), bf16[16,8,128]{2,1,0:T(8,128)(2,1)S(1)}, u32[]{:S(2)}, u32[]{:S(2)}) async-start(bf16[16,8,128]{2,1,0:T(8,128)(2,1)} %across.1), calls=%async_computation.1 | async-start | bytes 65536 | tf_op jit(solution)/shard_map/all_to_all | solution.py:427
  27.9 0.0 copy-done
  27.9 2.4 %waves.1 = (bf16[8,128,1024]{2,1,0:T(8,128)(2,1)S(1)}, f32[8,2,8,1024]{3,2,1,0:T(8,128)S(1)}, f32[8,2,4,1024]{3,2,1,0:T(4,128)S(1)}) custom-call(s32[1,1]{1,0:T(1,128)S(6)} %copy.10.live, s32[8,2,1024]{2,1,0:T(2,128)S(1)} %bitcast.6), custom_call_target="tpu_custom_call" | custom-call | flops 67108864 | bytes 3145728 | tf_op jit(solution)/shard_map/waves/pallas_call | solution.py:352
  30.3 3.5 %all-to-all-done.1.parts = bf16[16,8,128]{2,1,0:T(8,128)(2,1)S(1)} async-done(((bf16[16,8,128]{2,1,0:T(8,128)(2,1)}), bf16[16,8,128]{2,1,0:T(8,128)(2,1)S(1)}, u32[]{:S(2)}, u32[]{:S(2)}) %all-to-all-start.1) | async-done | bytes 32800 | tf_op jit(solution)/shard_map/all_to_all | solution.py:427
  33.9 1.5 %visibility.1 = f32[8,2,1024]{2,1,0:T(2,128)} custom-call(bf16[16,8,128]{2,1,0:T(8,128)(2,1)S(1)} %all-to-all-done.1.parts, bf16[8,128,1024]{2,1,0:T(8,128)(2,1)S(1)} %get-tuple-element.8.right, f32[8,2,8,1024]{3,2,1,0:T(8,128)S(1)} %get-tuple-element.9.near, f32[8,2,4,1024]{3,2,1,0:T(4,128)S(1)} %get-tuple-element.10.far), custom_call_target="tpu_custom_call" | custom-call | flops 134217728 | bytes 1048576 | tf_op jit(solution)/shard_map/visibility/pallas_call | solution.py:402
Async XLA Ops:
  0.7 27.2 %copy-start = (s32[1,1,8,2,1024]{4,3,2,1,0:T(2,128)S(1)}, s32[1,1,8,2,1024]{4,3,2,1,0:T(2,128)}, u32[]{:S(2)}) copy-start(s32[1,1,8,2,1024]{4,3,2,1,0:T(2,128)} %param.13) | copy-start | bytes 196612
  4.5 18.0 %all-to-all-start = ((bf16[32,17,2,128]{3,2,1,0:T(2,128)(2,1)}), bf16[32,17,2,128]{3,2,1,0:T(2,128)(2,1)S(1)}, u32[]{:S(2)}, u32[]{:S(2)}) async-start(bf16[32,17,2,128]{3,2,1,0:T(2,128)(2,1)} %bitcast.7), calls=%async_computation | async-start | bytes 557056 | tf_op jit(solution)/shard_map/all_to_all | solution.py:422
  23.7 10.1 %all-to-all-start.1 = ((bf16[16,8,128]{2,1,0:T(8,128)(2,1)}), bf16[16,8,128]{2,1,0:T(8,128)(2,1)S(1)}, u32[]{:S(2)}, u32[]{:S(2)}) async-start(bf16[16,8,128]{2,1,0:T(8,128)(2,1)} %across.1), calls=%async_computation.1 | async-start | bytes 65536 | tf_op jit(solution)/shard_map/all_to_all | solution.py:427

commit v8 on v6

--- a/solution.py
+++ b/solution.py
@@ -16,9 +16,7 @@
 NTOT = 65536
 UV_STEPS = 4096
 VMEM_LIMIT = 16 << 20
-CHUNK = 512
-CHAIN = 16
-AHEAD = 4
+CHUNK = 2048
 BF16 = jnp.bfloat16
 F32 = jnp.float32
 I32 = jnp.int32
@@ -51,18 +49,18 @@
     return groups, S // TILE // groups, inside
 
 
-def along_kernel(facets, cols, chunk, scal, offsets, names, strip, out, held, table, total, state, outside, small, sems):
+def along_kernel(facets, cols, chunk, scal, offsets, names, strip, out, held, table, total, outside, small, sems):
     count = held.shape[1]
     steps = count // chunk
     slots = names.shape[2]
-    copies = []
+    copies = {}
     notes = []
     for n, (src, dst) in enumerate(zip((offsets, names), small)):
         notes.append(pltpu.make_async_copy(src, dst, sems.at[steps + n]))
         notes[n].start()
-    for n in range(steps):
+    for n in reversed(range(steps)):
         part = pl.ds(n * chunk, chunk)
-        copies.append(pltpu.make_async_copy(strip.at[:, part], held.at[:, part], sems.at[n]))
+        copies[n] = pltpu.make_async_copy(strip.at[:, part], held.at[:, part], sems.at[n])
         copies[n].start()
     row_start = scal[0]
     rows = S // facets
@@ -92,71 +90,52 @@
         x, y = factors[n]
         return x * cosine - y * sine, y * cosine + x * sine
 
-    factor_tables(1, W, W, 1.0)
-    factor_tables(2, CHAIN * W, CHAIN * W, 1.0)
-    notes[0].wait()
-    col_start = small[0][0, 0] + lax.axis_index("col") * count
     factor_tables(
         0,
-        col_start + lax.broadcasted_iota(I32, (8, W), 1),
-        col_start + lax.broadcasted_iota(I32, (blocks, W), 1),
+        lax.broadcasted_iota(I32, (8, W), 1),
+        lax.broadcasted_iota(I32, (blocks, W), 1),
         1.0 / math.sqrt(L),
     )
-
-    def fill(n):
-        slot = n % (AHEAD + 1)
+    factor_tables(1, W, W, 1.0)
+    factor_tables(2, chunk, chunk, 1.0)
+    for k in range(blocks):
+        c1, s1 = factor(0, k)
+        turn_c, turn_s = factor(1, k)
+        twice = turn_c + turn_c
+        for local in range(chunk // W):
+            if local == 1:
+                c0, s0 = c1, s1
+                c1, s1 = c0 * turn_c - s0 * turn_s, s0 * turn_c + c0 * turn_s
+            elif local:
+                c0, c1 = c1, twice * c1 - c0
+                s0, s1 = s1, twice * s1 - s0
+            at = slice(local * W, (local + 1) * W)
+            table[8 * k : 8 * k + 8, at] = c1.astype(BF16)
+            table[S + 8 * k : S + 8 * k + 8, at] = s1.astype(BF16)
+    for n in reversed(range(steps)):
+        copies[n].wait()
+        if n == 0:
+            notes[0].wait()
+            col_start = small[0][0, 0] + lax.axis_index("col") * count
+            factor_tables(3, col_start, col_start, 1.0)
+        part = slice(n * chunk, (n + 1) * chunk)
+        cells = jnp.concatenate([held[0, part, :], held[1, part, :]], axis=1)
+        upper = jnp.dot(table[0:S, :], cells, preferred_element_type=F32)
+        lower = jnp.dot(table[S : 2 * S, :], cells, preferred_element_type=F32)
         for k in range(blocks):
             at = slice(8 * k, 8 * k + 8)
-            twice = None
-            for local in range(chunk // W):
-                stage = (n * (chunk // W) + local) % CHAIN
-                if stage == 0:
-                    if n == 0:
-                        c1, s1 = factor(0, k)
-                    else:
-                        leap_c, leap_s = factor(2, k)
-                        c0, s0 = state[4, at], state[5, at]
-                        c1, s1 = c0 * leap_c - s0 * leap_s, s0 * leap_c + c0 * leap_s
-                    if (n + 1) * chunk < count:
-                        state[4, at], state[5, at] = c1, s1
-                elif stage == 1:
-                    turn_c, turn_s = factor(1, k)
-                    twice = turn_c + turn_c
-                    state[6, at] = twice
-                    c0, s0 = c1, s1
-                    c1, s1 = c0 * turn_c - s0 * turn_s, s0 * turn_c + c0 * turn_s
-                else:
-                    if twice is None:
-                        twice = state[6, at]
-                        c0, s0, c1, s1 = (state[i, at] for i in range(4))
-                    c0, c1 = c1, twice * c1 - c0
-                    s0, s1 = s1, twice * s1 - s0
-                place = slice(local * W, (local + 1) * W)
-                table[slot, at, place] = c1.astype(BF16)
-                table[slot, S + 8 * k : S + 8 * k + 8, place] = s1.astype(BF16)
-            if (n + 1) * (chunk // W) % CHAIN:
-                for i, value in enumerate((c0, s0, c1, s1)):
-                    state[i, at] = value
-
-    ahead = min(AHEAD, steps)
-    for n in range(ahead):
-        fill(n)
-    for copy in copies:
-        copy.wait()
-    for n in range(steps):
-        if n + ahead < steps:
-            fill(n + ahead)
-        part = slice(n * chunk, (n + 1) * chunk)
-        cells = jnp.concatenate([held[0, part, :], held[1, part, :]], axis=1)
-        term = jnp.dot(table[n % (AHEAD + 1)], cells, preferred_element_type=F32)
-        if n == 0:
-            total[...] = term
-        else:
-            total[...] += term
-    real = total[0:S, 0:W] + total[S : 2 * S, W : 2 * W]
-    imag = total[0:S, W : 2 * W] - total[S : 2 * S, 0:W]
-    total[0:S, 0:W] = real
-    total[0:S, W : 2 * W] = imag
+            re = upper[at, 0:W] + lower[at, W : 2 * W]
+            im = upper[at, W : 2 * W] - lower[at, 0:W]
+            if n + 1 < steps:
+                old_re, old_im = total[at, 0:W], total[at, W : 2 * W]
+                leap_c, leap_s = factor(2, k)
+                re = re + (old_re * leap_c + old_im * leap_s)
+                im = im + (old_im * leap_c - old_re * leap_s)
+            if n == 0:
+                turn_c, turn_s = factor(3, k)
+                re, im = re * turn_c + im * turn_s, im * turn_c - re * turn_s
+            total[at, 0:W] = re
+            total[at, W : 2 * W] = im
     notes[1].wait()
     across = small[0][0, 1]
     spot = lax.broadcasted_iota(I32, (2, W), 1)
@@ -186,10 +165,9 @@
         out_specs=pl.BlockSpec(memory_space=pltpu.VMEM),
         scratch_shapes=[
             pltpu.VMEM((2, count, W), BF16),
-            pltpu.VMEM((AHEAD + 1, 2 * S, chunk), BF16),
-            pltpu.VMEM((2 * S, 2 * W), F32),
-            pltpu.VMEM((7, S, W), F32),
-            pltpu.VMEM((6, S // 8, W), F32),
+            pltpu.VMEM((2 * S, chunk), BF16),
+            pltpu.VMEM((S, 2 * W), F32),
+            pltpu.VMEM((8, S // 8, W), F32),
             [
                 pltpu.SMEM(facet_offsets.shape, I32),
                 pltpu.SMEM(names.shape, I32),

time: 35.8 us -> 35.5 us (level)
  no operation moved by 1% of the time
where the time goes in v8:
time: 35.5 us; the launch traced here: 35.2 us
  waiting for transfers between devices  13.4 us (38%)
  starting transfers between devices  10.8 us (30%)
  Pallas kernels  9.02 us (25%)
  between operations  2 us (6%)
    all_to_all x1, waiting for transfers between devices, shards(): got = lax.all_to_all(pairs, ('facet', 'col'), 0, 0, tiled=True)  9.86 us
    all_to_all x1, starting transfers between devices, shards(): got = lax.all_to_all(pairs, ('facet', 'col'), 0, 0, tiled=True)  7.33 us
    all_to_all x1, waiting for transfers between devices, shards(): parts = lax.all_to_all(asked, 'facet', 0, 0, tiled=True)  3.52 us
    pallas_call x1, Pallas kernels, along(): pl.pallas_call(functools.partial(along_kernel, facets, cols, chunk), out_...  3.5 us
    all_to_all x1, starting transfers between devices, shards(): parts = lax.all_to_all(asked, 'facet', 0, 0, tiled=True)  3.5 us
    pallas_call x1, Pallas kernels, waves(): pl.pallas_call(functools.partial(waves_kernel, facets), out_shape=(jax.Sh...  2.42 us
    pallas_call x1, Pallas kernels, visibilities_of(): pl.pallas_call(functools.partial(visibility_kernel, facets), out_shape=ja...  1.46 us
    pallas_call x1, Pallas kernels, across(): pl.pallas_call(functools.partial(across_kernel, facets, cols), out_shape=...  1.23 us
  transfers between devices with their start and end apart: 2, of which 2 were waited for; matrix products, arithmetic and copies ran while one was open for 0% of the time, Pallas kernels for 8%

profile of v8, /device:TPU:0, one launch (start us, length us, event | category | flops | bytes accessed | tf_op | source)
XLA Modules:
  0.0 35.2 jit_solution(14820039775389239637)
XLA Ops:
  0.7 0.0 copy-start
  0.7 3.5 %along.1 = bf16[1088,128]{1,0:T(8,128)(2,1)} custom-call(s32[1]{0:T(128)S(6)} %copy.9.scal, s32[1,2]{1,0:T(1,128)} %offsets.1, s32[1,1,8]{2,1,0:T(1,128)} %names.1, bf16[2,4096,128]{2,1,0:T(8,128)(2,1)} %bitcast.8), custom_call_target="tpu_custom_call" | custom-call | flops 1073741824 | bytes 2097152 | tf_op jit(solution)/shard_map/along/pallas_call | solution.py:160
  4.2 7.3 %all-to-all-start = ((bf16[32,17,2,128]{3,2,1,0:T(2,128)(2,1)}), bf16[32,17,2,128]{3,2,1,0:T(2,128)(2,1)S(1)}, u32[]{:S(2)}, u32[]{:S(2)}) async-start(bf16[32,17,2,128]{3,2,1,0:T(2,128)(2,1)} %bitcast.7), calls=%async_computation | async-start | bytes 557056 | tf_op jit(solution)/shard_map/all_to_all | solution.py:398
  12.2 0.4 %base.1.right = bf16[256,512]{1,0:T(8,128)(2,1)S(1)} custom-call(s32[1]{0:T(128)S(6)} %copy.8.columns), custom_call_target="tpu_custom_call" | custom-call | flops 16777216 | bytes 262144 | tf_op jit(solution)/shard_map/base/pallas_call | solution.py:199
  12.6 9.9 %all-to-all-done = bf16[32,17,2,128]{3,2,1,0:T(2,128)(2,1)S(1)} async-done(((bf16[32,17,2,128]{3,2,1,0:T(2,128)(2,1)}), bf16[32,17,2,128]{3,2,1,0:T(2,128)(2,1)S(1)}, u32[]{:S(2)}, u32[]{:S(2)}) %all-to-all-start) | async-done | bytes 278560 | tf_op jit(solution)/shard_map/all_to_all | solution.py:398
  22.4 1.2 %across.1 = bf16[16,8,128]{2,1,0:T(8,128)(2,1)} custom-call(s32[1]{0:T(128)S(6)} %copy.8.columns, bf16[1088,128]{1,0:T(8,128)(2,1)S(1)} %bitcast.5, bf16[256,512]{1,0:T(8,128)(2,1)S(1)} %base.1.right), custom_call_target="tpu_custom_call" | custom-call | flops 134217728 | bytes 1048576 | tf_op jit(solution)/shard_map/across/pallas_call | solution.py:277
  23.7 3.5 %all-to-all-start.1 = ((bf16[16,8,128]{2,1,0:T(8,128)(2,1)}), bf16[16,8,128]{2,1,0:T(8,128)(2,1)S(1)}, u32[]{:S(2)}, u32[]{:S(2)}) async-start(bf16[16,8,128]{2,1,0:T(8,128)(2,1)} %across.1), calls=%async_computation.1 | async-start | bytes 65536 | tf_op jit(solution)/shard_map/all_to_all | solution.py:403
  27.8 0.0 copy-done
  27.8 2.4 %waves.1 = (bf16[8,128,1024]{2,1,0:T(8,128)(2,1)S(1)}, f32[8,2,8,1024]{3,2,1,0:T(8,128)S(1)}, f32[8,2,4,1024]{3,2,1,0:T(4,128)S(1)}) custom-call(s32[1,1]{1,0:T(1,128)S(6)} %copy.10.live, s32[8,2,1024]{2,1,0:T(2,128)S(1)} %bitcast.6), custom_call_target="tpu_custom_call" | custom-call | flops 67108864 | bytes 3145728 | tf_op jit(solution)/shard_map/waves/pallas_call | solution.py:328
  30.3 3.5 %all-to-all-done.1.parts = bf16[16,8,128]{2,1,0:T(8,128)(2,1)S(1)} async-done(((bf16[16,8,128]{2,1,0:T(8,128)(2,1)}), bf16[16,8,128]{2,1,0:T(8,128)(2,1)S(1)}, u32[]{:S(2)}, u32[]{:S(2)}) %all-to-all-start.1) | async-done | bytes 32800 | tf_op jit(solution)/shard_map/all_to_all | solution.py:403
  33.8 1.5 %visibility.1 = f32[8,2,1024]{2,1,0:T(2,128)} custom-call(bf16[16,8,128]{2,1,0:T(8,128)(2,1)S(1)} %all-to-all-done.1.parts, bf16[8,128,1024]{2,1,0:T(8,128)(2,1)S(1)} %get-tuple-element.8.right, f32[8,2,8,1024]{3,2,1,0:T(8,128)S(1)} %get-tuple-element.9.near, f32[8,2,4,1024]{3,2,1,0:T(4,128)S(1)} %get-tuple-element.10.far), custom_call_target="tpu_custom_call" | custom-call | flops 134217728 | bytes 1048576 | tf_op jit(solution)/shard_map/visibility/pallas_call | solution.py:378
Async XLA Ops:
  0.7 27.2 %copy-start = (s32[1,1,8,2,1024]{4,3,2,1,0:T(2,128)S(1)}, s32[1,1,8,2,1024]{4,3,2,1,0:T(2,128)}, u32[]{:S(2)}) copy-start(s32[1,1,8,2,1024]{4,3,2,1,0:T(2,128)} %param.13) | copy-start | bytes 196612
  4.2 18.3 %all-to-all-start = ((bf16[32,17,2,128]{3,2,1,0:T(2,128)(2,1)}), bf16[32,17,2,128]{3,2,1,0:T(2,128)(2,1)S(1)}, u32[]{:S(2)}, u32[]{:S(2)}) async-start(bf16[32,17,2,128]{3,2,1,0:T(2,128)(2,1)} %bitcast.7), calls=%async_computation | async-start | bytes 557056 | tf_op jit(solution)/shard_map/all_to_all | solution.py:398
  23.7 10.1 %all-to-all-start.1 = ((bf16[16,8,128]{2,1,0:T(8,128)(2,1)}), bf16[16,8,128]{2,1,0:T(8,128)(2,1)S(1)}, u32[]{:S(2)}, u32[]{:S(2)}) async-start(bf16[16,8,128]{2,1,0:T(8,128)(2,1)} %across.1), calls=%async_computation.1 | async-start | bytes 65536 | tf_op jit(solution)/shard_map/all_to_all | solution.py:403

commit v9 on v8

--- a/solution.py
+++ b/solution.py
@@ -217,25 +217,22 @@
     column = lax.axis_index("col")
     sources = []
     for f in range(facets):
-        parts = []
-        for part in range(2):
-            at = f * cols * size + part * rows
-            value = got[at : at + rows, :].astype(F32)
-            for h in range(1, cols):
-                value = value + got[at + h * size : at + h * size + rows, :].astype(F32)
-            parts.append(value)
-        re, im = parts
-        left[f * rows : (f + 1) * rows, 0:W] = re
-        left[f * rows : (f + 1) * rows, W : 2 * W] = im
-        left[height + f * rows : height + (f + 1) * rows, 0:W] = im
-        left[height + f * rows : height + (f + 1) * rows, W : 2 * W] = -re
+        for h in range(cols):
+            at = (f * cols + h) * size
+            re, im = got[at : at + rows, :], got[at + rows : at + 2 * rows, :]
+            near, far = slice(2 * h * W, (2 * h + 1) * W), slice((2 * h + 1) * W, (2 * h + 2) * W)
+            left[f * rows : (f + 1) * rows, near] = re
+            left[f * rows : (f + 1) * rows, far] = im
+            left[height + f * rows : height + (f + 1) * rows, near] = im
+            left[height + f * rows : height + (f + 1) * rows, far] = -re
         note = None
         for h in range(cols):
             at = (f * cols + h) * size + 2 * rows
             value = jnp.where(column == h, got[at : at + 2, :].astype(F32)[0:1], 0.0)
             note = value if note is None else note + value
         sources.append(note)
-    summed[...] = jnp.dot(left[...].astype(BF16), right[...], preferred_element_type=F32)
+    table = jnp.concatenate([right[...]] * cols, axis=0)
+    summed[...] = jnp.dot(left[...], table, preferred_element_type=F32)
     heads = jnp.concatenate(sources, axis=0)
     offset = (heads[:, W - 2 : W - 1] * 256.0 + heads[:, W - 1 : W]).astype(I32)
     lane = lax.broadcasted_iota(I32, (facets, wide), 1)
@@ -284,7 +281,7 @@
         ],
         out_specs=pl.BlockSpec(memory_space=pltpu.VMEM),
         scratch_shapes=[
-            pltpu.VMEM((2 * S, 2 * W), F32),
+            pltpu.VMEM((2 * S, 2 * W * cols), BF16),
             pltpu.VMEM((2 * S, 2 * S), F32),
             pltpu.VMEM((2, facets, 2 * S), F32),
         ],

time: 35.5 us -> 35.6 us (level)
  no operation moved by 1% of the time
where the time goes in v9:
time: 35.6 us; the launch traced here: 35.3 us
  waiting for transfers between devices  13.4 us (38%)
  starting transfers between devices  10.8 us (30%)
  Pallas kernels  9.12 us (26%)
  between operations  2 us (6%)
    all_to_all x1, waiting for transfers between devices, shards(): got = lax.all_to_all(pairs, ('facet', 'col'), 0, 0, tiled=True)  9.86 us
    all_to_all x1, starting transfers between devices, shards(): got = lax.all_to_all(pairs, ('facet', 'col'), 0, 0, tiled=True)  7.33 us
    all_to_all x1, waiting for transfers between devices, shards(): parts = lax.all_to_all(asked, 'facet', 0, 0, tiled=True)  3.52 us
    pallas_call x1, Pallas kernels, along(): pl.pallas_call(functools.partial(along_kernel, facets, cols, chunk), out_...  3.5 us
    all_to_all x1, starting transfers between devices, shards(): parts = lax.all_to_all(asked, 'facet', 0, 0, tiled=True)  3.5 us
    pallas_call x1, Pallas kernels, waves(): pl.pallas_call(functools.partial(waves_kernel, facets), out_shape=(jax.Sh...  2.42 us
    pallas_call x1, Pallas kernels, visibilities_of(): pl.pallas_call(functools.partial(visibility_kernel, facets), out_shape=ja...  1.46 us
    pallas_call x1, Pallas kernels, across(): pl.pallas_call(functools.partial(across_kernel, facets, cols), out_shape=...  1.33 us
  transfers between devices with their start and end apart: 2, of which 2 were waited for; matrix products, arithmetic and copies ran while one was open for 0% of the time, Pallas kernels for 8%

profile of v9, /device:TPU:0, one launch (start us, length us, event | category | flops | bytes accessed | tf_op | source)
XLA Modules:
  0.0 35.3 jit_solution(17338648187656750145)
XLA Ops:
  0.7 0.0 copy-start
  0.7 3.5 %along.1 = bf16[1088,128]{1,0:T(8,128)(2,1)} custom-call(s32[1]{0:T(128)S(6)} %copy.9.scal, s32[1,2]{1,0:T(1,128)} %offsets.1, s32[1,1,8]{2,1,0:T(1,128)} %names.1, bf16[2,4096,128]{2,1,0:T(8,128)(2,1)} %bitcast.8), custom_call_target="tpu_custom_call" | custom-call | flops 1073741824 | bytes 2097152 | tf_op jit(solution)/shard_map/along/pallas_call | solution.py:160
  4.2 7.3 %all-to-all-start = ((bf16[32,17,2,128]{3,2,1,0:T(2,128)(2,1)}), bf16[32,17,2,128]{3,2,1,0:T(2,128)(2,1)S(1)}, u32[]{:S(2)}, u32[]{:S(2)}) async-start(bf16[32,17,2,128]{3,2,1,0:T(2,128)(2,1)} %bitcast.7), calls=%async_computation | async-start | bytes 557056 | tf_op jit(solution)/shard_map/all_to_all | solution.py:395
  12.2 0.4 %base.1.right = bf16[256,512]{1,0:T(8,128)(2,1)S(1)} custom-call(s32[1]{0:T(128)S(6)} %copy.8.columns), custom_call_target="tpu_custom_call" | custom-call | flops 16777216 | bytes 262144 | tf_op jit(solution)/shard_map/base/pallas_call | solution.py:199
  12.6 9.9 %all-to-all-done = bf16[32,17,2,128]{3,2,1,0:T(2,128)(2,1)S(1)} async-done(((bf16[32,17,2,128]{3,2,1,0:T(2,128)(2,1)}), bf16[32,17,2,128]{3,2,1,0:T(2,128)(2,1)S(1)}, u32[]{:S(2)}, u32[]{:S(2)}) %all-to-all-start) | async-done | bytes 278560 | tf_op jit(solution)/shard_map/all_to_all | solution.py:395
  22.4 1.3 %across.1 = bf16[16,8,128]{2,1,0:T(8,128)(2,1)} custom-call(s32[1]{0:T(128)S(6)} %copy.8.columns, bf16[1088,128]{1,0:T(8,128)(2,1)S(1)} %bitcast.5, bf16[256,512]{1,0:T(8,128)(2,1)S(1)} %base.1.right), custom_call_target="tpu_custom_call" | custom-call | flops 134217728 | bytes 1048576 | tf_op jit(solution)/shard_map/across/pallas_call | solution.py:274
  23.8 3.5 %all-to-all-start.1 = ((bf16[16,8,128]{2,1,0:T(8,128)(2,1)}), bf16[16,8,128]{2,1,0:T(8,128)(2,1)S(1)}, u32[]{:S(2)}, u32[]{:S(2)}) async-start(bf16[16,8,128]{2,1,0:T(8,128)(2,1)} %across.1), calls=%async_computation.1 | async-start | bytes 65536 | tf_op jit(solution)/shard_map/all_to_all | solution.py:400
  27.9 0.0 copy-done
  27.9 2.4 %waves.1 = (bf16[8,128,1024]{2,1,0:T(8,128)(2,1)S(1)}, f32[8,2,8,1024]{3,2,1,0:T(8,128)S(1)}, f32[8,2,4,1024]{3,2,1,0:T(4,128)S(1)}) custom-call(s32[1,1]{1,0:T(1,128)S(6)} %copy.10.live, s32[8,2,1024]{2,1,0:T(2,128)S(1)} %bitcast.6), custom_call_target="tpu_custom_call" | custom-call | flops 67108864 | bytes 3145728 | tf_op jit(solution)/shard_map/waves/pallas_call | solution.py:325
  30.4 3.5 %all-to-all-done.1.parts = bf16[16,8,128]{2,1,0:T(8,128)(2,1)S(1)} async-done(((bf16[16,8,128]{2,1,0:T(8,128)(2,1)}), bf16[16,8,128]{2,1,0:T(8,128)(2,1)S(1)}, u32[]{:S(2)}, u32[]{:S(2)}) %all-to-all-start.1) | async-done | bytes 32800 | tf_op jit(solution)/shard_map/all_to_all | solution.py:400
  33.9 1.5 %visibility.1 = f32[8,2,1024]{2,1,0:T(2,128)} custom-call(bf16[16,8,128]{2,1,0:T(8,128)(2,1)S(1)} %all-to-all-done.1.parts, bf16[8,128,1024]{2,1,0:T(8,128)(2,1)S(1)} %get-tuple-element.8.right, f32[8,2,8,1024]{3,2,1,0:T(8,128)S(1)} %get-tuple-element.9.near, f32[8,2,4,1024]{3,2,1,0:T(4,128)S(1)} %get-tuple-element.10.far), custom_call_target="tpu_custom_call" | custom-call | flops 134217728 | bytes 1048576 | tf_op jit(solution)/shard_map/visibility/pallas_call | solution.py:375
Async XLA Ops:
  0.7 27.3 %copy-start = (s32[1,1,8,2,1024]{4,3,2,1,0:T(2,128)S(1)}, s32[1,1,8,2,1024]{4,3,2,1,0:T(2,128)}, u32[]{:S(2)}) copy-start(s32[1,1,8,2,1024]{4,3,2,1,0:T(2,128)} %param.13) | copy-start | bytes 196612
  4.2 18.3 %all-to-all-start = ((bf16[32,17,2,128]{3,2,1,0:T(2,128)(2,1)}), bf16[32,17,2,128]{3,2,1,0:T(2,128)(2,1)S(1)}, u32[]{:S(2)}, u32[]{:S(2)}) async-start(bf16[32,17,2,128]{3,2,1,0:T(2,128)(2,1)} %bitcast.7), calls=%async_computation | async-start | bytes 557056 | tf_op jit(solution)/shard_map/all_to_all | solution.py:395
  23.8 10.1 %all-to-all-start.1 = ((bf16[16,8,128]{2,1,0:T(8,128)(2,1)}), bf16[16,8,128]{2,1,0:T(8,128)(2,1)S(1)}, u32[]{:S(2)}, u32[]{:S(2)}) async-start(bf16[16,8,128]{2,1,0:T(8,128)(2,1)} %across.1), calls=%async_computation.1 | async-start | bytes 65536 | tf_op jit(solution)/shard_map/all_to_all | solution.py:400

commit v10 on v9

--- a/solution.py
+++ b/solution.py
@@ -342,7 +342,7 @@
 
 def visibility_kernel(facets, parts, right, near, far, out, held):
     groups, _, inside = split(facets)
-    slots = out.shape[0]
+    slots, vis = out.shape[0], out.shape[2]
     sources = facets // groups
     for f in range(sources):
         held[f] = parts[f].astype(F32)
@@ -355,19 +355,20 @@
         y = pltpu.roll(x, W // 2, 1)
         both = [jnp.where(lane < W // 2, x, y), jnp.where(lane < W // 2, y, x)][:inside]
         lhs = [z * sign for z in both] + [pltpu.roll(z, TILE, 1) for z in both]
-        middle = jnp.dot(
-            jnp.concatenate(lhs, axis=0).astype(BF16), right[j], preferred_element_type=F32
-        )
-        real, imag = middle[0:8], middle[TILE : TILE + 8]
-        for h in range(1, 4):
-            more_re = middle[8 * h : 8 * h + 8]
-            more_im = middle[TILE + 8 * h : TILE + 8 * h + 8]
-            cosine, sine = far[j, 0, h : h + 1, :], far[j, 1, h : h + 1, :]
-            real = real + (cosine * more_re - sine * more_im)
-            imag = imag + (cosine * more_im + sine * more_re)
-        cosine, sine = near[j, 0], near[j, 1]
-        out[j, 0:1, :] = jnp.sum(cosine * real - sine * imag, axis=0, keepdims=True)
-        out[j, 1:2, :] = jnp.sum(cosine * imag + sine * real, axis=0, keepdims=True)
+        lhs = jnp.concatenate(lhs, axis=0).astype(BF16)
+        for at in range(0, vis, vis // 2):
+            cut = slice(at, at + vis // 2)
+            middle = jnp.dot(lhs, right[j, :, cut], preferred_element_type=F32)
+            real, imag = middle[0:8], middle[TILE : TILE + 8]
+            for h in range(1, 4):
+                more_re = middle[8 * h : 8 * h + 8]
+                more_im = middle[TILE + 8 * h : TILE + 8 * h + 8]
+                cosine, sine = far[j, 0, h : h + 1, cut], far[j, 1, h : h + 1, cut]
+                real = real + (cosine * more_re - sine * more_im)
+                imag = imag + (cosine * more_im + sine * more_re)
+            cosine, sine = near[j, 0, :, cut], near[j, 1, :, cut]
+            out[j, 0:1, cut] = jnp.sum(cosine * real - sine * imag, axis=0, keepdims=True)
+            out[j, 1:2, cut] = jnp.sum(cosine * imag + sine * real, axis=0, keepdims=True)
 
 
 def visibilities_of(parts, tables, facets):

time: 35.6 us -> 35.6 us (level)
  no operation moved by 1% of the time
where the time goes in v10:
time: 35.6 us; the launch traced here: 35.3 us
  waiting for transfers between devices  13.4 us (38%)
  starting transfers between devices  10.8 us (30%)
  Pallas kernels  9.12 us (26%)
  between operations  2 us (6%)
    all_to_all x1, waiting for transfers between devices, shards(): got = lax.all_to_all(pairs, ('facet', 'col'), 0, 0, tiled=True)  9.86 us
    all_to_all x1, starting transfers between devices, shards(): got = lax.all_to_all(pairs, ('facet', 'col'), 0, 0, tiled=True)  7.33 us
    all_to_all x1, waiting for transfers between devices, shards(): parts = lax.all_to_all(asked, 'facet', 0, 0, tiled=True)  3.52 us
    pallas_call x1, Pallas kernels, along(): pl.pallas_call(functools.partial(along_kernel, facets, cols, chunk), out_...  3.5 us
    all_to_all x1, starting transfers between devices, shards(): parts = lax.all_to_all(asked, 'facet', 0, 0, tiled=True)  3.5 us
    pallas_call x1, Pallas kernels, waves(): pl.pallas_call(functools.partial(waves_kernel, facets), out_shape=(jax.Sh...  2.42 us
    pallas_call x1, Pallas kernels, visibilities_of(): pl.pallas_call(functools.partial(visibility_kernel, facets), out_shape=ja...  1.45 us
    pallas_call x1, Pallas kernels, across(): pl.pallas_call(functools.partial(across_kernel, facets, cols), out_shape=...  1.33 us
  transfers between devices with their start and end apart: 2, of which 2 were waited for; matrix products, arithmetic and copies ran while one was open for 0% of the time, Pallas kernels for 8%

profile of v10, /device:TPU:0, one launch (start us, length us, event | category | flops | bytes accessed | tf_op | source)
XLA Modules:
  0.0 35.3 jit_solution(8397900544902188302)
XLA Ops:
  0.7 0.0 copy-start
  0.7 3.5 %along.1 = bf16[1088,128]{1,0:T(8,128)(2,1)} custom-call(s32[1]{0:T(128)S(6)} %copy.9.scal, s32[1,2]{1,0:T(1,128)} %offsets.1, s32[1,1,8]{2,1,0:T(1,128)} %names.1, bf16[2,4096,128]{2,1,0:T(8,128)(2,1)} %bitcast.8), custom_call_target="tpu_custom_call" | custom-call | flops 1073741824 | bytes 2097152 | tf_op jit(solution)/shard_map/along/pallas_call | solution.py:160
  4.2 7.3 %all-to-all-start = ((bf16[32,17,2,128]{3,2,1,0:T(2,128)(2,1)}), bf16[32,17,2,128]{3,2,1,0:T(2,128)(2,1)S(1)}, u32[]{:S(2)}, u32[]{:S(2)}) async-start(bf16[32,17,2,128]{3,2,1,0:T(2,128)(2,1)} %bitcast.7), calls=%async_computation | async-start | bytes 557056 | tf_op jit(solution)/shard_map/all_to_all | solution.py:396
  12.2 0.4 %base.1.right = bf16[256,512]{1,0:T(8,128)(2,1)S(1)} custom-call(s32[1]{0:T(128)S(6)} %copy.8.columns), custom_call_target="tpu_custom_call" | custom-call | flops 16777216 | bytes 262144 | tf_op jit(solution)/shard_map/base/pallas_call | solution.py:199
  12.6 9.9 %all-to-all-done = bf16[32,17,2,128]{3,2,1,0:T(2,128)(2,1)S(1)} async-done(((bf16[32,17,2,128]{3,2,1,0:T(2,128)(2,1)}), bf16[32,17,2,128]{3,2,1,0:T(2,128)(2,1)S(1)}, u32[]{:S(2)}, u32[]{:S(2)}) %all-to-all-start) | async-done | bytes 278560 | tf_op jit(solution)/shard_map/all_to_all | solution.py:396
  22.4 1.3 %across.1 = bf16[16,8,128]{2,1,0:T(8,128)(2,1)} custom-call(s32[1]{0:T(128)S(6)} %copy.8.columns, bf16[1088,128]{1,0:T(8,128)(2,1)S(1)} %bitcast.5, bf16[256,512]{1,0:T(8,128)(2,1)S(1)} %base.1.right), custom_call_target="tpu_custom_call" | custom-call | flops 134217728 | bytes 1048576 | tf_op jit(solution)/shard_map/across/pallas_call | solution.py:274
  23.8 3.5 %all-to-all-start.1 = ((bf16[16,8,128]{2,1,0:T(8,128)(2,1)}), bf16[16,8,128]{2,1,0:T(8,128)(2,1)S(1)}, u32[]{:S(2)}, u32[]{:S(2)}) async-start(bf16[16,8,128]{2,1,0:T(8,128)(2,1)} %across.1), calls=%async_computation.1 | async-start | bytes 65536 | tf_op jit(solution)/shard_map/all_to_all | solution.py:401
  27.9 0.0 copy-done
  27.9 2.4 %waves.1 = (bf16[8,128,1024]{2,1,0:T(8,128)(2,1)S(1)}, f32[8,2,8,1024]{3,2,1,0:T(8,128)S(1)}, f32[8,2,4,1024]{3,2,1,0:T(4,128)S(1)}) custom-call(s32[1,1]{1,0:T(1,128)S(6)} %copy.10.live, s32[8,2,1024]{2,1,0:T(2,128)S(1)} %bitcast.6), custom_call_target="tpu_custom_call" | custom-call | flops 67108864 | bytes 3145728 | tf_op jit(solution)/shard_map/waves/pallas_call | solution.py:325
  30.4 3.5 %all-to-all-done.1.parts = bf16[16,8,128]{2,1,0:T(8,128)(2,1)S(1)} async-done(((bf16[16,8,128]{2,1,0:T(8,128)(2,1)}), bf16[16,8,128]{2,1,0:T(8,128)(2,1)S(1)}, u32[]{:S(2)}, u32[]{:S(2)}) %all-to-all-start.1) | async-done | bytes 32800 | tf_op jit(solution)/shard_map/all_to_all | solution.py:401
  33.9 1.5 %visibility.1 = f32[8,2,1024]{2,1,0:T(2,128)} custom-call(bf16[16,8,128]{2,1,0:T(8,128)(2,1)S(1)} %all-to-all-done.1.parts, bf16[8,128,1024]{2,1,0:T(8,128)(2,1)S(1)} %get-tuple-element.8.right, f32[8,2,8,1024]{3,2,1,0:T(8,128)S(1)} %get-tuple-element.9.near, f32[8,2,4,1024]{3,2,1,0:T(4,128)S(1)} %get-tuple-element.10.far), custom_call_target="tpu_custom_call" | custom-call | flops 134217728 | bytes 1048576 | tf_op jit(solution)/shard_map/visibility/pallas_call | solution.py:376
Async XLA Ops:
  0.7 27.3 %copy-start = (s32[1,1,8,2,1024]{4,3,2,1,0:T(2,128)S(1)}, s32[1,1,8,2,1024]{4,3,2,1,0:T(2,128)}, u32[]{:S(2)}) copy-start(s32[1,1,8,2,1024]{4,3,2,1,0:T(2,128)} %param.13) | copy-start | bytes 196612
  4.2 18.3 %all-to-all-start = ((bf16[32,17,2,128]{3,2,1,0:T(2,128)(2,1)}), bf16[32,17,2,128]{3,2,1,0:T(2,128)(2,1)S(1)}, u32[]{:S(2)}, u32[]{:S(2)}) async-start(bf16[32,17,2,128]{3,2,1,0:T(2,128)(2,1)} %bitcast.7), calls=%async_computation | async-start | bytes 557056 | tf_op jit(solution)/shard_map/all_to_all | solution.py:396
  23.8 10.1 %all-to-all-start.1 = ((bf16[16,8,128]{2,1,0:T(8,128)(2,1)}), bf16[16,8,128]{2,1,0:T(8,128)(2,1)S(1)}, u32[]{:S(2)}, u32[]{:S(2)}) async-start(bf16[16,8,128]{2,1,0:T(8,128)(2,1)} %across.1), calls=%async_computation.1 | async-start | bytes 65536 | tf_op jit(solution)/shard_map/all_to_all | solution.py:401
